TPU v7x, 256 devices: a whole 4x4x8 slice. The times are simulated.
256 devices in a mesh: rep: 16 (over z_hi, x), tp: 16 (over z_lo, y, core).
Axes of the slice: x: 4, y: 4, z: 8 (z_hi: 4, z_lo: 2; z = z_hi * 2 + z_lo), core: 2. Of those that a mesh axis runs over, the one named last changes fastest.
Arguments:
- tokens: bfloat16 [512, 4096], P(('rep', 'tp')), may hold values from -6 to 6
- conv_state: bfloat16 [3, 512, 8192], P(None, 'rep', 'tp'), may hold values from -6 to 6
- ssm_state: float32 [512, 16, 8192], P('rep', None, 'tp'), may hold values from -6 to 6
- norm_gains: bfloat16 [2, 4096], P(None, ('rep', 'tp')), may hold values from 0.5 to 1.5
- conv_weight: bfloat16 [4, 8192], P(None, ('rep', 'tp')), may hold values from -3 to 3
- conv_skip: bfloat16 [2, 8192], P(None, ('rep', 'tp')), may hold values from -3 to 3
- step_bias: bfloat16 [8192], P(('rep', 'tp')), may hold values from -5 to -1
- decay_log: bfloat16 [16, 8192], P(None, ('rep', 'tp')), may hold values from 0 to 2.796875
- input_proj: bfloat16 [4096, 2, 8192], P(('rep', 'tp')), may hold values from -0.09375 to 0.09375
- select_proj: bfloat16 [8192, 288], P('tp', 'rep'), may hold values from -0.0625 to 0.0625
- step_proj: bfloat16 [256, 8192], P(('rep', 'tp')), may hold values from -0.375 to 0.375
- output_proj: bfloat16 [8192, 4096], P(None, ('rep', 'tp')), may hold values from -0.0625 to 0.0625
- router: bfloat16 [4096, 16], P(('rep', 'tp')), may hold values from -0.09375 to 0.09375
- expert_proj: bfloat16 [4096, 2, 2, 12288], P(('rep', 'tp')), may hold values from -0.09375 to 0.09375
- expert_ids: int32 [512, 2], P(('rep', 'tp')), may hold values from 0 to 15, as said below
Outputs:
- mamba_out: bfloat16 [512, 4096], P(('rep', 'tp'))
- conv_next: bfloat16 [3, 512, 8192], P(None, 'rep', 'tp')
- ssm_next: float32 [512, 16, 8192], P('rep', None, 'tp')
- expert_hidden: bfloat16 [1024, 12288], P('rep', 'tp')
Inputs may be any that keep to these rules, and one draw needn't show every extreme that they name: `expert_ids`: each row names two different experts. Within each aligned block of 2 rows (the rows of one device) each expert e < 2 is named by at most 2 rows.
All inputs are finite; a program needn't handle non-finite values.
Results may differ from a plain program's by a relative error of at most 0.04.
Values may be sent and summed in bfloat16 or wider, within the bound.
A program may use at most 128 MiB of HBM per device.

v0:
```python
import math

import jax
import jax.numpy as jnp
from jax import lax
from jax.sharding import Mesh
from jax.sharding import PartitionSpec as P

CAPACITY = 2
REP_TP = ("rep_0", "rep_1", "tp")
REP = ("rep_0", "rep_1")


epsilon = 1e-05


def in_one_piece(arrays, axis, dim, along):
    widths = [a.shape[along] for a in arrays]
    both = jnp.concatenate(arrays, axis=along)
    out = lax.all_gather(both, axis, axis=dim, tiled=True)
    return tuple(jnp.split(out, [sum(widths[:k]) for k in range(1, len(widths))], axis=along))


def from_everyone(array, axis):
    devices = lax.axis_size(axis)
    return lax.all_to_all(
        jnp.broadcast_to(array[None], (devices, *array.shape)), axis, 0, 0, tiled=True
    )


def joined_along(blocks, dim):
    dims = list(blocks.shape[1:])
    dims[dim] *= blocks.shape[0]
    return jnp.moveaxis(blocks, 0, dim).reshape(dims)


def gathered_copies(array, axis, dim):
    blocks = from_everyone(array, axis)
    return joined_along(blocks, dim)


def gather_packed(arrays, axis, dims):
    ravelled = jnp.concatenate([a.reshape(-1) for a in arrays])
    lines, at, outs = (lax.all_gather(ravelled, axis), 0, [])
    for a, dim in zip(arrays, dims):
        blocks = lines[:, at : at + a.size].reshape(-1, *a.shape)
        outs.append(joined_along(blocks, dim))
        at += a.size
    return tuple(outs)


def over_copies(array, axis):
    return from_everyone(array, axis).astype(jnp.float32).sum(axis=0)


def split_up(array, dim, devices):
    before, after = (array.shape[:dim], array.shape[dim + 1 :])
    return jnp.moveaxis(array.reshape(*before, devices, -1, *after), dim, 0)


def sent_and_summed(array, axis, dim):
    devices = lax.axis_size(axis)
    blocks = lax.all_to_all(split_up(array, dim, devices), axis, 0, 0, tiled=True)
    return jnp.sum(blocks.astype(jnp.float32), axis=0)


def side_by_side(arrays, axis, dim, along):
    widths = [math.prod(a.shape[along:]) for a in arrays]
    both = jnp.concatenate(
        [a.reshape(*a.shape[:along], w) for a, w in zip(arrays, widths)], axis=along
    )
    out = lax.all_gather(both, axis, axis=dim, tiled=True)
    blocks = jnp.split(out, [sum(widths[:k]) for k in range(1, len(widths))], axis=along)
    return tuple((b.reshape(*out.shape[:along], *a.shape[along:]) for a, b in zip(arrays, blocks)))


def own_block(blocks, axes, order):
    dims = [lax.axis_size(a) for a in axes]
    blocks = blocks.reshape(*dims, *blocks.shape[1:])
    blocks = blocks.transpose(*order, *range(len(axes), blocks.ndim))
    blocks = blocks.reshape(-1, *blocks.shape[len(axes) :])
    for k in order:
        blocks = lax.psum_scatter(blocks, axes[k], scatter_dimension=0, tiled=True)
    return blocks[0]


def scatter_axes(array, axes, order, dim):
    devices = lax.axis_size(axes)
    return own_block(split_up(array, dim, devices), axes, order)


def norm_scale(values, gain):
    mean_square = jnp.mean(values * values, axis=-1, keepdims=True)
    return values * lax.rsqrt(mean_square + epsilon) * gain.astype(jnp.float32)


def shards(
    tokens,
    conv_state,
    ssm_state,
    norm_gains,
    conv_weight,
    conv_skip,
    step_bias,
    decay_log,
    input_proj,
    select_proj,
    step_proj,
    output_proj,
    router,
    expert_proj,
    expert_ids,
):
    tp_count = lax.axis_size("tp")
    tp_index = lax.axis_index("tp")
    norm_gain, conv_taps, skip_rows, shift_full, decay_full, router_full = (
        lax.all_gather(norm_gains, REP_TP, axis=1, tiled=True),
        *in_one_piece((conv_weight, conv_skip), REP_TP, 1, 0),
        lax.all_gather(step_bias, REP_TP, axis=0, tiled=True),
        lax.all_gather(decay_log, REP_TP, axis=1, tiled=True),
        lax.all_gather(router, REP_TP, axis=0, tiled=True),
    )
    inner_dev = ssm_state.shape[2]
    channel_start = tp_index * inner_dev
    conv_taps = lax.dynamic_slice_in_dim(conv_taps, channel_start, inner_dev, 1).astype(jnp.float32)
    skip_rows = lax.dynamic_slice_in_dim(skip_rows, channel_start, inner_dev, 1).astype(jnp.float32)
    shift_dev = lax.dynamic_slice_in_dim(shift_full, channel_start, inner_dev, 0).astype(
        jnp.float32
    )
    decay_dev = lax.dynamic_slice_in_dim(decay_full, channel_start, inner_dev, 1).astype(
        jnp.float32
    )
    model_rows = input_proj.shape[0]
    inner_all = input_proj.shape[2]
    input_blocks, expert_blocks, step_blocks = (
        lax.all_to_all(
            input_proj.reshape(model_rows, 1, 2, inner_all),
            "tp",
            split_axis=3,
            concat_axis=0,
            tiled=True,
        ),
        lax.all_to_all(expert_proj, "tp", split_axis=3, concat_axis=0, tiled=True),
        lax.all_to_all(
            step_proj.reshape(step_proj.shape[0], 1, 1, inner_all),
            "tp",
            split_axis=3,
            concat_axis=0,
            tiled=True,
        ),
    )
    output_blocks = lax.all_to_all(output_proj, "tp", split_axis=0, concat_axis=1, tiled=True)
    residual_in = tokens.astype(jnp.float32)
    normed = norm_scale(residual_in, norm_gain[0]).astype(jnp.bfloat16)
    features = gathered_copies(normed, "tp", 0)
    shard_piece = lax.all_gather(input_blocks, REP, axis=0, tiled=True)
    piece_rows = shard_piece.shape[0]
    projected = jnp.dot(
        features, shard_piece.reshape(piece_rows, 2 * inner_dev), preferred_element_type=jnp.float32
    )
    output_rows, step_rows, select_rows = gather_packed(
        (output_blocks, step_blocks, select_proj), REP, (1, 0, 1)
    )
    step_rows = step_rows.reshape(step_rows.shape[0], inner_dev)
    step_rank = step_rows.shape[0]
    state_count = ssm_state.shape[1]
    conv_input = projected[:, :inner_dev]
    gate_z = projected[:, inner_dev:]
    history = conv_state.astype(jnp.float32)
    conv_mix = (
        jnp.sum(conv_taps[:-1, None, :] * history, axis=0)
        + conv_taps[-1] * conv_input
        + skip_rows[0]
    )
    conv_next = jnp.concatenate([conv_state[1:], conv_input.astype(jnp.bfloat16)[None]], axis=0)
    activated = jax.nn.silu(conv_mix)
    select_part = jnp.dot(
        activated.astype(jnp.bfloat16), select_rows, preferred_element_type=jnp.float32
    )
    selected = over_copies(select_part.astype(jnp.bfloat16), "tp").astype(jnp.float32)
    step_low = selected[:, :step_rank].astype(jnp.bfloat16)
    input_map = selected[:, step_rank : step_rank + state_count]
    output_map = selected[:, step_rank + state_count :]
    step_size = jax.nn.softplus(
        jnp.dot(step_low, step_rows, preferred_element_type=jnp.float32) + shift_dev
    )
    decay_rate = -jnp.exp(decay_dev)
    factor = jnp.exp(step_size[:, None, :] * decay_rate[None])
    ssm_next = factor * ssm_state + (step_size * activated)[:, None, :] * input_map[:, :, None]
    readout = jnp.sum(ssm_next * output_map[:, :, None], axis=1) + skip_rows[1] * activated
    gated_out = (readout * jax.nn.silu(gate_z)).astype(jnp.bfloat16)
    output_part = jnp.dot(gated_out, output_rows, preferred_element_type=jnp.float32)
    mixer_out = sent_and_summed(output_part.astype(jnp.bfloat16), "tp", 0)
    residual = residual_in + mixer_out
    mamba_out = residual.astype(jnp.bfloat16)
    moe_in = norm_scale(residual, norm_gain[1]).astype(jnp.bfloat16)
    logits = jnp.dot(moe_in, router_full, preferred_element_type=jnp.float32)
    expert_total = logits.shape[1]
    choose = (
        expert_ids[:, :, None] == jnp.arange(expert_total, dtype=jnp.int32)[None, None, :]
    ).astype(jnp.float32)
    picked = jnp.sum(choose * logits[:, None, :], axis=2)
    first_gate = jax.nn.sigmoid(picked[:, 0] - picked[:, 1])
    second_gate = jax.nn.sigmoid(picked[:, 1] - picked[:, 0])
    window_count = expert_blocks.shape[1]
    window = jnp.arange(window_count, dtype=jnp.int32)
    names_first = expert_ids[:, 0:1] == window[None, :]
    names_second = expert_ids[:, 1:2] == window[None, :]
    zero = jnp.zeros((), jnp.float32)
    gate_w = jnp.where(names_first, first_gate[:, None], zero) + jnp.where(
        names_second, second_gate[:, None], zero
    )
    routed = (names_first | names_second).astype(jnp.int32)
    position = jnp.cumsum(routed, axis=0) - routed
    slot_of = (position[:, :, None] == jnp.arange(CAPACITY, dtype=jnp.int32)[None, None, :]) & (
        routed[:, :, None] > 0
    )
    slot_x = jnp.einsum(
        "tec,td->ecd", slot_of.astype(jnp.bfloat16), moe_in, preferred_element_type=jnp.float32
    )
    slot_local = window_count * CAPACITY
    slot_x = slot_x.astype(jnp.bfloat16).reshape(slot_local, moe_in.shape[1])
    slot_gate = (
        jnp.einsum("tec,te->ec", slot_of.astype(jnp.float32), gate_w)
        .astype(jnp.bfloat16)
        .reshape(slot_local)
    )
    feature_rows = expert_blocks.shape[0]
    replica_rows, gate_all = side_by_side((slot_x, slot_gate), "tp", 0, 1)
    gathered = lax.all_to_all(replica_rows, REP, split_axis=1, concat_axis=0, tiled=True)
    hidden_dev = expert_blocks.shape[3]
    group_rows = tp_count * slot_local
    picked_rows = gathered
    picked_rows = picked_rows.reshape(
        group_rows * lax.axis_size(REP) // slot_local, window_count, CAPACITY, feature_rows
    )
    product = jnp.einsum(
        "gecd,dexf->gecxf", picked_rows, expert_blocks, preferred_element_type=jnp.float32
    )
    summed = scatter_axes(
        product.reshape(group_rows * lax.axis_size(REP), 2 * hidden_dev).astype(jnp.bfloat16),
        REP,
        (1, 0),
        0,
    ).astype(jnp.float32)
    hidden = (
        gate_all.astype(jnp.float32)[:, None]
        * jax.nn.silu(summed[:, :hidden_dev])
        * summed[:, hidden_dev:]
    )
    expert_hidden = hidden.astype(jnp.bfloat16)
    return (mamba_out, conv_next, ssm_next, expert_hidden)


def solution(mesh):
    split = Mesh(mesh.devices.reshape(4, 4, mesh.shape["tp"]), ("rep_0", "rep_1", "tp"))
    return jax.shard_map(
        shards,
        mesh=split,
        in_specs=(
            P(REP_TP, None),
            P(None, REP, "tp"),
            P(REP, None, "tp"),
            P(None, REP_TP),
            P(None, REP_TP),
            P(None, REP_TP),
            P(REP_TP),
            P(None, REP_TP),
            P(REP_TP, None, None),
            P("tp", REP),
            P(REP_TP, None),
            P(None, REP_TP),
            P(REP_TP, None),
            P(REP_TP, None, None, None),
            P(REP_TP, None),
        ),
        out_specs=(P(REP_TP, None), P(None, REP, "tp"), P(REP, None, "tp"), P(REP, "tp")),
        check_vma=False,
    )
```

profile of v0, /device:TPU:2, one launch (start us, length us, event | category | flops | bytes accessed | tf_op | source)
XLA Modules:
  0.0 1967.1 jit_solution(4106802272947335639)
XLA Ops:
  7.2 8.3 copy.135
  16.0 62.6 %reduce.12 = bf16[8192]{0:T(1024)(128)(2,1)S(1)} reduce(bf16[8192,1,1,1]{3,2,1,0:T(2,128)(2,1)} %bitcast.104, bf16[]{:T(256)} %broadcast.160), dimensions={1,2,3}, to_apply=%bitcast.77.reduce_sub_computation | reduce | bytes 32770
  95.3 8.4 reshape.274
  103.7 62.0 %bitcast_reduce_fusion = bf16[8192]{0:T(1024)(128)(2,1)S(1)} fusion(bf16[8192,1,1,1]{3,2,1,0:T(2,128)(2,1)} %reshape.274), kind=kLoop, calls=%fused_computation.72 | loop fusion | bytes 32768 | tf_op jit(solution)/shard_map/all_to_all | solution.py:144
  169.9 6.8 copy.129
  176.6 7.7 bitcast_bitcast_fusion
  190.1 18.9 all_to_all.92
  213.1 10.3 copy.152
  223.4 333.8 %all-gather.2 = bf16[256,16,2]{1,2,0:T(2,128)(2,1)S(1)} all-gather(bf16[1,16,2]{1,2,0:T(2,128)(2,1)S(1)} %bitcast.128), channel_id=1, replica_groups=mesh['rep_0'=4,'rep_1'=4,'tp'=16] {'rep_0','rep_1','tp'}, dimensions={0}, use_global_device_ids=true | all-gather | bytes 16448 | tf_op jit(solution)/shard_map/all_gather | solution.py:117
  562.2 342.0 %all-gather.1 = bf16[256,32,6]{1,2,0:T(8,128)(2,1)S(1)} all-gather(bf16[1,32,6]{1,2,0:T(8,128)(2,1)S(1)} %maximum_bitcast_fusion.1), channel_id=1, replica_groups=mesh['rep_0'=4,'rep_1'=4,'tp'=16] {'rep_0','rep_1','tp'}, dimensions={0}, use_global_device_ids=true | all-gather | bytes 98688 | tf_op jit(solution)/shard_map/all_gather | solution.py:20
  917.3 11.3 copy.132
  928.6 6.0 fusion.24
  939.2 343.9 %all-gather.3 = bf16[256,32,16]{1,2,0:T(8,128)(2,1)S(1)} all-gather(bf16[1,32,16]{1,2,0:T(8,128)(2,1)S(1)} %bitcast.126), channel_id=1, replica_groups=mesh['rep_0'=4,'rep_1'=4,'tp'=16] {'rep_0','rep_1','tp'}, dimensions={0}, use_global_device_ids=true | all-gather | bytes 263168 | tf_op jit(solution)/shard_map/all_gather | solution.py:120
  1284.8 91.6 %all-reduce = bf16[8192]{0:T(1024)(128)(2,1)S(1)} all-reduce(bf16[8192]{0:T(1024)(128)(2,1)S(1)} %dynamic-update-slice), channel_id=1, replica_groups=mesh['rep_0'=4,'rep_1'=4,'tp'=16] {'rep_0','rep_1','tp'}, use_global_device_ids=true, to_apply=%add | all-reduce | flops 8192 | bytes 32768
  1386.3 6.5 copy.139
  1404.5 20.2 %copy.142 = bf16[16,2,2,12288]{0,2,1,3:T(2,128)(2,1)} copy(bf16[16,2,2,12288]{3,2,1,0:T(2,128)(2,1)S(1)} %copy-done.1) | data formatting | bytes 3145728 | tf_op args[13]
  1424.6 17.7 reshape.277
  1442.3 328.0 %all_gather.34 = bf16[4096,16]{1,0:T(8,128)(2,1)S(1)} all-gather(bf16[16,16]{1,0:T(8,128)(2,1)S(1)} %copy-done.10), channel_id=1, replica_groups=mesh['rep_0'=4,'rep_1'=4,'tp'=16] {'rep_0','rep_1','tp'}, dimensions={0}, use_global_device_ids=true | all-gather | bytes 131584 | tf_op jit(solution)/shard_map/all_gather | solution.py:121
  1776.3 32.2 %all-gather.4 = bf16[16,4,4097]{2,1,0:T(4,128)(2,1)S(1)} all-gather(bf16[1,4,4097]{2,1,0:T(4,128)(2,1)S(1)} %maximum_bitcast_fusion), channel_id=1, replica_groups=mesh['rep_0'=4,'rep_1'=4,'tp'=16] {'tp'}, dimensions={0}, use_global_device_ids=true | all-gather | bytes 557192 | tf_op jit(solution)/shard_map/all_gather | solution.py:72
  1809.8 25.0 %all-to-all-start.6 = ((bf16[64,16,256]{2,0,1:T(8,128)(2,1)}), bf16[64,16,256]{2,0,1:T(8,128)(2,1)S(1)}, u32[]{:S(2)}, u32[]{:S(2)}) async-start(bf16[64,16,256]{2,0,1:T(8,128)(2,1)} %bitcast.95), calls=%async_computation.6 | async-start | bytes 1048576 | tf_op jit(solution)/shard_map/all_to_all | solution.py:230
  1834.9 12.1 reshape.278
  1847.0 26.5 %copy.143 = bf16[16,2,2,16,768]{4,0,3,2,1:T(8,128)(2,1)S(1)} copy(bf16[16,2,2,16,768]{0,2,1,4,3:T(2,128)(2,1)} %bitcast.98) | data formatting | bytes 3145728 | tf_op jit(solution)/shard_map/all_to_all | solution.py:143
  1885.3 39.0 %reduce-scatter.3.cloned.1.call-done = bf16[4,64,1536]{2,1,0:T(8,128)(2,1)} async-done(((bf16[16,64,1536]{2,1,0:T(8,128)(2,1)}), bf16[4,64,1536]{2,1,0:T(8,128)(2,1)}) %reduce-scatter.3.cloned.1.call-update) | async-done | bytes 786448 | tf_op jit(solution)/shard_map/reduce_scatter | solution.py:83
  1925.7 32.7 %reduce-scatter.5.cloned.1.call-done = bf16[1,64,1536]{2,1,0:T(8,128)(2,1)} async-done(((bf16[4,64,1536]{2,1,0:T(8,128)(2,1)}), bf16[1,64,1536]{2,1,0:T(8,128)(2,1)}) %reduce-scatter.5.cloned.1.call-update) | async-done | bytes 196624 | tf_op jit(solution)/shard_map/reduce_scatter | solution.py:83
  (139 shorter events, 99.0 us)
Async XLA Ops:
  7.2 78.0 %copy-start.6 = (bf16[8192,16]{0,1:T(8,128)(2,1)S(1)}, bf16[8192,16]{0,1:T(8,128)(2,1)}, u32[]{:S(2)}) copy-start(bf16[8192,16]{0,1:T(8,128)(2,1)} %param.26) | copy-start | bytes 786436
  7.2 78.7 %copy-start.7 = (bf16[512,18]{0,1:T(8,128)(2,1)S(1)}, bf16[512,18]{0,1:T(8,128)(2,1)}, u32[]{:S(2)}) copy-start(bf16[512,18]{0,1:T(8,128)(2,1)} %param.24) | copy-start | bytes 55300
  79.2 12.0 all-to-all-start.3
  91.2 74.5 %all-to-all-start.2 = ((bf16[16,512,16]{1,2,0:T(8,128)(2,1)}), bf16[16,512,16]{1,2,0:T(8,128)(2,1)S(1)}, u32[]{:S(2)}, u32[]{:S(2)}) async-start(bf16[16,512,16]{1,2,0:T(8,128)(2,1)} %bitcast.96), calls=%async_computation.2 | async-start | bytes 524288 | tf_op jit(solution)/shard_map/all_to_all | solution.py:152
  94.8 810.3 %all-gather.10.cloned.1.call-start = ((), (), s32[]{:S(2)}) async-start(), calls=%async_computation.13 | async-start | bytes 5048320 | tf_op jit(solution)/shard_map/all_gather | solution.py:44
  103.7 66.2 %copy-start.3 = (bf16[16,2,8192]{2,1,0:T(2,128)(2,1)S(1)}, bf16[16,2,8192]{2,1,0:T(2,128)(2,1)}, u32[]{:S(2)}) copy-start(bf16[16,2,8192]{2,1,0:T(2,128)(2,1)} %param.23) | copy-start | bytes 1572868
  169.8 747.5 %all-gather.8.cloned.1.call-start = ((), (), s32[]{:S(2)}) async-start(), calls=%async_computation.10 | async-start | bytes 8912896 | tf_op jit(solution)/shard_map/all_gather | solution.py:156
  209.0 14.5 copy-start.12
  209.0 348.5 %copy-start.5 = (bf16[2,4096]{1,0:T(2,128)(2,1)S(1)}, bf16[2,4096]{1,0:T(2,128)(2,1)}, u32[]{:S(2)}) copy-start(bf16[2,4096]{1,0:T(2,128)(2,1)} %param.15) | copy-start | bytes 49156
  213.1 349.1 %copy-start.11 = (bf16[4,32]{1,0:T(4,128)(2,1)S(1)}, bf16[4,32]{1,0:T(4,128)(2,1)}, u32[]{:S(2)}) copy-start(bf16[4,32]{1,0:T(4,128)(2,1)} %param.19) | copy-start | bytes 772
  213.1 349.1 %copy-start.13 = (bf16[2,32]{1,0:T(2,128)(2,1)S(1)}, bf16[2,32]{1,0:T(2,128)(2,1)}, u32[]{:S(2)}) copy-start(bf16[2,32]{1,0:T(2,128)(2,1)} %param.20) | copy-start | bytes 388
  213.1 691.7 %copy-start.4 = (bf16[3,32,512]{2,1,0:T(8,128)(2,1)S(1)}, bf16[3,32,512]{2,1,0:T(8,128)(2,1)}, u32[]{:S(2)}) copy-start(bf16[3,32,512]{2,1,0:T(8,128)(2,1)} %param.16) | copy-start | bytes 294916
  558.7 346.2 %all-to-all-start = ((bf16[16,2,4096]{2,1,0:T(2,128)(2,1)}), bf16[16,2,4096]{2,1,0:T(2,128)(2,1)S(1)}, u32[]{:S(2)}, u32[]{:S(2)}) async-start(bf16[16,2,4096]{2,1,0:T(2,128)(2,1)} %broadcast_in_dim.24), calls=%async_computation | async-start | bytes 524288 | tf_op jit(solution)/shard_map/all_to_all | solution.py:26
  934.6 349.9 %copy-start.14 = (bf16[32]{0:T(256)(128)(2,1)S(1)}, bf16[32]{0:T(256)(128)(2,1)}, u32[]{:S(2)}) copy-start(bf16[32]{0:T(256)(128)(2,1)} %param.21) | copy-start | bytes 196
  934.6 441.8 %copy-start.8 = (s32[2,2]{1,0:T(2,128)S(1)}, s32[2,2]{1,0:T(2,128)}, u32[]{:S(2)}) copy-start(s32[2,2]{1,0:T(2,128)} %param.29) | copy-start | bytes 52
  935.7 457.2 %all-to-all-start.4 = ((bf16[16,32,288]{2,1,0:T(8,128)(2,1)}), bf16[16,32,288]{2,1,0:T(8,128)(2,1)S(1)}, u32[]{:S(2)}, u32[]{:S(2)}) async-start(bf16[16,32,288]{2,1,0:T(8,128)(2,1)} %broadcast_in_dim.25), calls=%async_computation.4 | async-start | bytes 786432 | tf_op jit(solution)/shard_map/all_to_all | solution.py:26
  1399.0 371.3 %all-to-all-start.5 = ((bf16[16,2,4096]{2,1,0:T(2,128)(2,1)}), bf16[16,2,4096]{2,1,0:T(2,128)(2,1)S(1)}, u32[]{:S(2)}, u32[]{:S(2)}) async-start(bf16[16,2,4096]{2,1,0:T(2,128)(2,1)} %reshape.243), calls=%async_computation.5 | async-start | bytes 524288 | tf_op jit(solution)/shard_map/all_to_all | solution.py:63
  1424.6 17.7 copy-start.10
  1770.3 39.5 %all-to-all-start.7 = ((bf16[16,2,24576]{2,1,0:T(2,128)(2,1)}), bf16[16,2,24576]{2,1,0:T(2,128)(2,1)S(1)}, u32[]{:S(2)}, u32[]{:S(2)}) async-start(bf16[16,2,24576]{2,1,0:T(2,128)(2,1)} %reshape.277), calls=%async_computation.7 | async-start | bytes 3145728 | tf_op jit(solution)/shard_map/all_to_all | solution.py:143
  1808.8 38.2 %copy-start = (bf16[64,4097]{1,0:T(8,128)(2,1)}, bf16[64,4097]{1,0:T(8,128)(2,1)S(1)}, u32[]{:S(2)}) copy-start(bf16[64,4097]{1,0:T(8,128)(2,1)S(1)} %reshape.261) | copy-start | bytes 1573252
  1809.8 63.7 %all-to-all-start.6 = ((bf16[64,16,256]{2,0,1:T(8,128)(2,1)}), bf16[64,16,256]{2,0,1:T(8,128)(2,1)S(1)}, u32[]{:S(2)}, u32[]{:S(2)}) async-start(bf16[64,16,256]{2,0,1:T(8,128)(2,1)} %bitcast.95), calls=%async_computation.6 | async-start | bytes 1048576 | tf_op jit(solution)/shard_map/all_to_all | solution.py:230
  1834.8 89.4 %reduce-scatter.3.cloned.1.call-start = ((), (), s32[]{:S(2)}) async-start(), calls=%async_computation.11 | async-start | bytes 3932160 | tf_op jit(solution)/shard_map/reduce_scatter | solution.py:83
  1881.3 42.9 %slice-start.1 = ((bf16[3,32,512]{2,1,0:T(8,128)(2,1)}), bf16[2,32,512]{2,1,0:T(8,128)(2,1)S(1)}, s32[]{:S(2)}) async-start(bf16[3,32,512]{2,1,0:T(8,128)(2,1)} %param.16), calls=%async_computation.15 | async-start | bytes 131072 | tf_op jit(solution)/shard_map/slice | solution.py:175
  1885.2 73.2 %reduce-scatter.5.cloned.1.call-start = ((), (), s32[]{:S(2)}) async-start(), calls=%async_computation.12 | async-start | bytes 983040 | tf_op jit(solution)/shard_map/reduce_scatter | solution.py:83
  (4 other events, 33.4 us)
Sparse Core Ops, SparseCore 0:
  169.9 81.1 all-gather.9
  254.1 112.3 all-gather.7
  1885.3 38.8 reduce-scatter.2
  1926.6 31.7 reduce-scatter.4
where the time goes:
time: 1980 us; the launch traced here: 1970 us
  blocking collectives  1490 us (75%)
  local copies, waits for them, and re-layouts  252 us (13%)
  waiting for transfers between devices  76.8 us (4%)
  other arithmetic  70.1 us (4%)
  starting transfers between devices  51.4 us (3%)
    all_gather x1, blocking collectives, shards(): lax.all_gather(decay_log, REP_TP, axis=1, tiled=True)  344 us
    all_gather x1, blocking collectives, in_one_piece(): out = lax.all_gather(both, axis, axis=dim, tiled=True)  342 us
    all_gather x1, blocking collectives, shards(): lax.all_gather(norm_gains, REP_TP, axis=1, tiled=True)  334 us
    all_gather x1, blocking collectives, shards(): lax.all_gather(router, REP_TP, axis=0, tiled=True)  328 us
    unnamed x1, blocking collectives  91.6 us
    unnamed x48, local copies, waits for them, and re-layouts  91.4 us
    reduce_scatter x2, waiting for transfers between devices, own_block(): blocks = lax.psum_scatter(blocks, axes[k], scatter_dimension=0, tiled=True)  71.6 us
    unnamed x3, other arithmetic  62.6 us
  transfers between devices with their start and end apart: 11, of which 3 were waited for; matrix products, arithmetic and copies ran while one was open for 11% of the time, Pallas kernels for 0%

commit v1 on v0

v1 whole, which is shorter than its diff:
```python
import functools

import jax
import jax.numpy as jnp
from jax import lax
from jax.experimental import pallas as pl
from jax.experimental.pallas import tpu as pltpu
from jax.sharding import Mesh
from jax.sharding import PartitionSpec as P

CAPACITY = 2
REP = ("rep_0", "rep_1")
REP_TP = ("rep_0", "rep_1", "tp")
MESH = pl.DeviceIdType.MESH
EPS = 1e-05
bf16 = jnp.bfloat16
f32 = jnp.float32
LANES = 128

PHASES = (
    "x1", "rs", "wi", "rg", "x2", "wo", "st", "prz", "sez", "prx",
    "sex", "pr2", "stz", "stx", "p3x", "p3z", "we", "sel", "gz", "gx",
    "mo", "mc", "y1", "info", "y2", "lx", "lz", "ex0", "ex1", "ex2",
    "ex3", "ez0", "ez1", "ez2", "ez3",
)
PH = {name: k for k, name in enumerate(PHASES)}


def sigmoid(v):
    return 1.0 / (1.0 + jnp.exp(-v))


def silu(v):
    return v / (1.0 + jnp.exp(-v))


def softplus(v):
    return jnp.maximum(v, 0.0) + jnp.log1p(jnp.exp(-jnp.abs(v)))


def dot(a, b):
    return jnp.dot(a, b, preferred_element_type=f32)


def dot_nt(a, b):
    return lax.dot_general(a, b, (((1,), (1,)), ((), ())), preferred_element_type=f32)


def kernel(
    nz, nx, nt,
    tokens, conv_state, ssm_state, input_proj, expert_proj, output_t, step_row, select_t, packed,
    router_gain, info,
    mamba_out, conv_next, ssm_next, expert_hidden,
    x_s, x1, x2, xx, rs_s, rs_r, wi_s, wi_r, rg_r, wo_r, st_s, st_r, st_b, st_z, st_x, pr_z, pr_x, pr2,
    se_z, se_x, p3, p3x, p3zs, p3z, we_s, we_r, sel_s, sel_r, maps, step_b, act_b, ro_b, ga_s, g_z, g_x,
    mo_s, mo_r, mc_r, y_s, y1, y2, yy, info_s, info_r, lg, lgx, lgzs, lgz, pe, pex, pezs, pez,
    ssem, rsem,
):
    nr = nz * nx
    z, x, t = lax.axis_index("rep_0"), lax.axis_index("rep_1"), lax.axis_index("tp")
    r = z * nx + x
    rows = input_proj.shape[0]
    fb = rows * nt
    ch = ssm_state.shape[2]
    st = ssm_state.shape[1]
    td = tokens.shape[0]
    rq = td * nt
    rank = nr * nt
    hid = expert_proj.shape[3] // nt
    groups = {
        "tp": (nt, t, lambda p: {"tp": p}),
        "rep": (nr, r, lambda p: {"rep_0": p // nx, "rep_1": p % nx}),
        "x": (nx, x, lambda p: {"rep_1": p}),
        "z": (nz, z, lambda p: {"rep_0": p}),
    }
    sent = []

    def send(group, name, src, dst):
        n, me, dev = groups[group]
        k = PH[name]

        def body(step, carry):
            peer = (me + step) % n
            pltpu.make_async_remote_copy(
                src_ref=src(peer), dst_ref=dst.at[me], send_sem=ssem.at[k], recv_sem=rsem.at[k],
                device_id=dev(peer), device_id_type=MESH,
            ).start()
            return carry

        lax.fori_loop(1, n, body, 0)
        pltpu.make_async_copy(src(me), dst.at[me], rsem.at[k]).start()
        sent.append((k, dst, n))

    def arrived(name, dst):
        pltpu.make_async_copy(dst, dst, rsem.at[PH[name]]).wait()

    def cols(ref, p, width):
        return ref.at[:, pl.ds(pl.multiple_of(p * width, width), width)]

    xv = tokens[...]
    for q in range(nr):
        x_s[q] = xv[:, q * fb : (q + 1) * fb]
    send("rep", "x1", lambda p: x_s.at[p], x1)
    xf = xv.astype(f32)
    rs = lax.rsqrt(jnp.mean(xf * xf, axis=1, keepdims=True) + EPS)
    rs_s[...] = jnp.broadcast_to(rs, (td, LANES))
    send("tp", "rs", lambda p: rs_s, rs_r)
    for j in range(2):
        wi_s[j * rows : (j + 1) * rows, :] = input_proj[:, j, :]
    send("tp", "wi", lambda p: cols(wi_s, p, ch), wi_r)
    send("tp", "rg", lambda p: router_gain, rg_r)
    send("z", "prz", lambda p: packed, pr_z)
    send("z", "sez", lambda p: select_t, se_z)
    arrived("x1", x1)
    send("tp", "x2", lambda p: x1, x2)
    at_row = lax.broadcasted_iota(jnp.int32, (nt, 1), 0) == t
    st_s[...] = jnp.where(at_row, step_row[...].astype(f32), 0.0).astype(bf16)
    send("tp", "st", lambda p: cols(st_s, p, ch), st_r)
    send("tp", "wo", lambda p: cols(output_t, p, ch), wo_r)
    arrived("prz", pr_z)
    send("x", "prx", lambda p: pr_z, pr_x)
    arrived("sez", se_z)
    send("x", "sex", lambda p: se_z, se_x)
    for e in range(2):
        for j in range(2):
            q = 2 * e + j
            we_s[q * rows : (q + 1) * rows, :] = expert_proj[:, e, j, :]

    arrived("rg", rg_r)
    rgv = rg_r[...].reshape(fb, LANES)
    rgt = rgv.astype(f32).T
    gain0 = rgt[16:17, :]
    gain1 = rgt[17:18, :]
    arrived("x2", x2)

    def place(src, gain, dst):
        def body(q, carry):
            block = src[:, q].reshape(rq, fb).astype(f32)
            dst[q % nx, q // nx] = (block * gain).astype(bf16)
            return carry

        lax.fori_loop(0, nr, body, 0)

    place(x2, gain0, xx)
    arrived("wi", wi_r)
    lhs = xx[...].reshape(nr * rq, fb)
    for j in range(2):
        w = wi_r[:, j * rows : (j + 1) * rows, :].reshape(fb, ch)
        p3[:, :, :, j * ch : (j + 1) * ch] = dot(lhs, w).astype(bf16).reshape(nx, nz, rq, ch)
    send("x", "p3x", lambda p: p3.at[p], p3x)
    send("tp", "we", lambda p: cols(we_s, p, hid), we_r)

    arrived("st", st_r)
    st_b[...] = jnp.sum(st_r[...].astype(f32), axis=0).astype(bf16)
    send("z", "stz", lambda p: st_b, st_z)
    arrived("prx", pr_x)
    send("tp", "pr2", lambda p: pr_x.at[p % nx, p // nx], pr2)
    arrived("stz", st_z)
    send("x", "stx", lambda p: st_z, st_x)
    arrived("sex", se_x)
    srw = select_t.shape[0]
    sp = sel_s.shape[1]
    width = (rank + 2 * st) // nr
    shape = (sp, nr * srw)
    at_col = lax.broadcasted_iota(jnp.int32, shape, 0)
    place_of = lax.broadcasted_iota(jnp.int32, shape, 1)
    blk, off = place_of // srw, place_of % srw
    true_col = ((blk % nz) * nx + blk // nz) * width + off
    perm = jnp.where((true_col == at_col) & (off < width), 1.0, 0.0).astype(bf16)
    select_all = dot(perm, se_x[...].reshape(nr * srw, ch)).astype(bf16)
    arrived("rs", rs_r)
    rsv = rs_r[...].reshape(rq, LANES)[:, 0:1]

    arrived("p3x", p3x)
    acc = p3x[0].astype(f32)
    for k in range(1, nx):
        acc = acc + p3x[k].astype(f32)
    p3zs[...] = acc.astype(bf16)
    send("z", "p3z", lambda p: p3zs.at[p], p3z)
    arrived("pr2", pr2)
    par = pr2[...].reshape(ch, LANES).astype(f32).T
    history = jnp.sum(par[0:3][:, None, :] * conv_state[...].astype(f32), axis=0) + par[4:5]
    decay_rate = -jnp.exp(par[7 : 7 + st])
    conv_next[0] = conv_state[1]
    conv_next[1] = conv_state[2]
    arrived("p3z", p3z)
    acc = p3z[0].astype(f32)
    for k in range(1, nz):
        acc = acc + p3z[k].astype(f32)
    projected = acc * rsv
    conv_input = projected[:, :ch]
    gate_z = projected[:, ch:]
    conv_next[2] = conv_input.astype(bf16)
    activated = silu(history + par[3:4] * conv_input)
    sel_s[...] = dot_nt(activated.astype(bf16), select_all).astype(bf16)
    send("tp", "sel", lambda p: sel_s, sel_r)
    arrived("stx", st_x)
    step_all = jnp.concatenate([st_x[q % nx, q // nx] for q in range(nr)], axis=0)
    act_b[...] = activated
    arrived("sel", sel_r)
    selected = jnp.sum(sel_r[...].astype(f32), axis=0)
    step_low = selected[:, :rank].astype(bf16)
    maps[...] = jnp.broadcast_to(selected[:, rank : rank + 2 * st][:, :, None], maps.shape)
    step_b[...] = softplus(dot(step_low, step_all) + par[6:7])

    def token(i, carry):
        s = step_b[pl.ds(i, 1), :]
        a = act_b[pl.ds(i, 1), :]
        m = maps[i]
        wide = jnp.concatenate([m] * (ch // LANES), axis=1)
        nxt = jnp.exp(s * decay_rate) * ssm_state[i] + (s * a) * wide[:st]
        ssm_next[i] = nxt
        ro_b[pl.ds(i, 1), :] = jnp.sum(nxt * wide[st:], axis=0, keepdims=True)
        return carry

    lax.fori_loop(0, rq, token, 0)
    readout = ro_b[...] + par[5:6] * activated
    ga_s[...] = (readout * silu(gate_z)).astype(bf16)

    send("z", "gz", lambda p: ga_s, g_z)
    arrived("gz", g_z)
    send("x", "gx", lambda p: g_z, g_x)
    arrived("wo", wo_r)
    arrived("gx", g_x)
    mo = dot_nt(g_x[...].reshape(nr * rq, ch), wo_r[...].reshape(fb, ch))
    mo_s[...] = mo.astype(bf16).reshape(nx, nz, nt, td, fb)
    send("rep", "mo", lambda p: mo_s.at[p % nx, p // nx], mo_r)
    arrived("mo", mo_r)
    send("tp", "mc", lambda p: mo_r.at[:, p], mc_r)
    arrived("mc", mc_r)
    acc = x_s[...].astype(f32)
    for k in range(nt):
        acc = acc + mc_r[k].astype(f32)
    y_s[...] = acc.astype(bf16)
    send("rep", "y1", lambda p: y_s.at[p], y1)
    square = jnp.sum(jnp.sum(acc * acc, axis=0), axis=1, keepdims=True)
    rs2 = lax.rsqrt(square * (1.0 / (nr * fb)) + EPS)
    lane = lax.broadcasted_iota(jnp.int32, (td, LANES), 1)
    info_s[...] = jnp.where(lane == 0, rs2, info[...])
    send("tp", "info", lambda p: info_s, info_r)
    for q in range(nr):
        mamba_out[:, q * fb : (q + 1) * fb] = y_s[q]

    arrived("y1", y1)
    send("tp", "y2", lambda p: y1, y2)
    arrived("we", we_r)
    arrived("y2", y2)
    place(y2, gain1, yy)
    lhs2 = yy[...].reshape(nr * rq, fb)
    lg[...] = dot(lhs2, rgv).astype(bf16).reshape(nx, nz, rq, LANES)
    send("x", "lx", lambda p: lg.at[p], lgx)
    for q in range(4):
        w = we_r[:, q * rows : (q + 1) * rows, :].reshape(fb, hid)
        pe[q] = dot(lhs2, w).astype(bf16).reshape(nx, nz, rq, hid)
        send("x", "ex%d" % q, lambda p, q=q: pe.at[q, p], pex.at[q])

    arrived("lx", lgx)
    acc = lgx[0].astype(f32)
    for k in range(1, nx):
        acc = acc + lgx[k].astype(f32)
    lgzs[...] = acc.astype(bf16)
    send("z", "lz", lambda p: lgzs.at[p], lgz)
    for q in range(4):
        arrived("ex%d" % q, pex.at[q])
        acc = pex[q, 0].astype(f32)
        for k in range(1, nx):
            acc = acc + pex[q, k].astype(f32)
        pezs[q] = acc.astype(bf16)
        send("z", "ez%d" % q, lambda p, q=q: pezs.at[q, p], pez.at[q])

    arrived("info", info_r)
    arrived("lz", lgz)
    acc = lgz[0].astype(f32)
    for k in range(1, nz):
        acc = acc + lgz[k].astype(f32)
    inf = info_r[...].reshape(rq, LANES)
    scale = inf[:, 0:1]
    id0, id1 = inf[:, 1:2], inf[:, 2:3]
    logits = acc * scale
    lane = lax.broadcasted_iota(jnp.int32, (rq, LANES), 1).astype(f32)
    zero = jnp.zeros((), f32)
    first = jnp.sum(jnp.where(lane == id0, logits, zero), axis=1, keepdims=True)
    second = jnp.sum(jnp.where(lane == id1, logits, zero), axis=1, keepdims=True)
    gate_first = sigmoid(first - second)
    gate_second = sigmoid(second - first)
    inft = inf.T
    slots = 2 * CAPACITY * nt
    slot = lax.broadcasted_iota(jnp.int32, (slots, rq), 0).astype(f32)
    token_at = lax.broadcasted_iota(jnp.int32, (slots, rq), 1)
    base = ((token_at // td) * (2 * CAPACITY)).astype(f32)
    total = jnp.zeros((slots, hid), f32)
    for e in range(2):
        gate = jnp.where(id0 == e, gate_first, zero) + jnp.where(id1 == e, gate_second, zero)
        gate = gate.astype(bf16).astype(f32)
        halves = []
        for j in range(2):
            q = 2 * e + j
            arrived("ez%d" % q, pez.at[q])
            acc = pez[q, 0].astype(f32)
            for k in range(1, nz):
                acc = acc + pez[q, k].astype(f32)
            halves.append(acc * scale)
        hidden = (gate * silu(halves[0]) * halves[1]).astype(bf16)
        want = inft[3 + e : 4 + e, :]
        pick = jnp.where((slot == base + want) & (want >= 0.0), 1.0, 0.0).astype(bf16)
        total = total + dot(pick, hidden)
    expert_hidden[...] = total.astype(bf16)

    for k, dst, n in sent:
        part = dst.at[pl.ds(0, n - 1)]
        pltpu.make_async_copy(part, part, ssem.at[k]).wait()


def shards(
    nz, nx, nt, tokens, conv_state, ssm_state, norm_gains, conv_weight, conv_skip, step_bias, decay_log,
    input_proj, select_proj, step_proj, output_proj, router, expert_proj, expert_ids,
):
    nr = nz * nx
    rows = input_proj.shape[0]
    td, model = tokens.shape
    rq = td * nt
    fb = rows * nt
    _, st, ch = ssm_state.shape
    hid = expert_proj.shape[3] // nt
    cdev = conv_weight.shape[1]

    packed = jnp.concatenate([conv_weight, conv_skip, step_bias[None], decay_log], axis=0).T
    packed = jnp.pad(packed, ((0, 0), (0, LANES - packed.shape[1])))
    router_gain = jnp.concatenate([router, norm_gains.T], axis=1)
    router_gain = jnp.pad(router_gain, ((0, 0), (0, LANES - router_gain.shape[1])))
    select_t = select_proj.T
    srw = -(-select_t.shape[0] // 16) * 16
    sp = -(-select_t.shape[0] * nr // LANES) * LANES
    select_t = jnp.pad(select_t, ((0, srw - select_t.shape[0]), (0, 0)))
    window = jnp.arange(2, dtype=jnp.int32)
    routed = ((expert_ids[:, 0:1] == window) | (expert_ids[:, 1:2] == window)).astype(jnp.int32)
    position = jnp.cumsum(routed, axis=0) - routed
    want = jnp.where(routed > 0, window * CAPACITY + position, -1)
    info = jnp.concatenate([jnp.zeros((td, 1), jnp.int32), expert_ids, want], axis=1).astype(f32)
    info = jnp.pad(info, ((0, 0), (0, LANES - info.shape[1])))

    V = pltpu.VMEM
    scratch = dict(
        x_s=((nr, td, fb), bf16), x1=((nr, td, fb), bf16), x2=((nt, nr, td, fb), bf16),
        xx=((nx, nz, rq, fb), bf16),
        rs_s=((td, LANES), f32), rs_r=((nt, td, LANES), f32),
        wi_s=((2 * rows, nt * ch), bf16), wi_r=((nt, 2 * rows, ch), bf16),
        rg_r=((nt, rows, LANES), bf16),
        wo_r=((nt, output_proj.shape[1], ch), bf16),
        st_s=((nt, nt * ch), bf16), st_r=((nt, nt, ch), bf16), st_b=((nt, ch), bf16),
        st_z=((nz, nt, ch), bf16), st_x=((nx, nz, nt, ch), bf16),
        pr_z=((nz, cdev, LANES), bf16), pr_x=((nx, nz, cdev, LANES), bf16), pr2=((nt, cdev, LANES), bf16),
        se_z=((nz, srw, ch), bf16), se_x=((nx, nz, srw, ch), bf16),
        p3=((nx, nz, rq, 2 * ch), bf16), p3x=((nx, nz, rq, 2 * ch), bf16),
        p3zs=((nz, rq, 2 * ch), bf16), p3z=((nz, rq, 2 * ch), bf16),
        we_s=((4 * rows, nt * hid), bf16), we_r=((nt, 4 * rows, hid), bf16),
        sel_s=((rq, sp), bf16), sel_r=((nt, rq, sp), bf16),
        maps=((rq, 2 * st, LANES), f32), step_b=((rq, ch), f32), act_b=((rq, ch), f32),
        ro_b=((rq, ch), f32),
        ga_s=((rq, ch), bf16), g_z=((nz, rq, ch), bf16), g_x=((nx, nz, rq, ch), bf16),
        mo_s=((nx, nz, nt, td, fb), bf16), mo_r=((nr, nt, td, fb), bf16),
        mc_r=((nt, nr, td, fb), bf16), y_s=((nr, td, fb), bf16), y1=((nr, td, fb), bf16),
        y2=((nt, nr, td, fb), bf16), yy=((nx, nz, rq, fb), bf16),
        info_s=((td, LANES), f32), info_r=((nt, td, LANES), f32),
        lg=((nx, nz, rq, LANES), bf16), lgx=((nx, nz, rq, LANES), bf16),
        lgzs=((nz, rq, LANES), bf16), lgz=((nz, rq, LANES), bf16),
        pe=((4, nx, nz, rq, hid), bf16), pex=((4, nx, nz, rq, hid), bf16),
        pezs=((4, nz, rq, hid), bf16), pez=((4, nz, rq, hid), bf16),
    )
    scratch_shapes = [V(s, d) for s, d in scratch.values()]
    scratch_shapes += [pltpu.SemaphoreType.DMA((len(PHASES),))] * 2
    operands = (
        tokens, conv_state, ssm_state, input_proj, expert_proj, output_proj.T, step_proj, select_t, packed,
        router_gain, info,
    )
    return pl.pallas_call(
        functools.partial(kernel, nz, nx, nt),
        out_shape=(
            jax.ShapeDtypeStruct((td, model), bf16),
            jax.ShapeDtypeStruct(conv_state.shape, bf16),
            jax.ShapeDtypeStruct(ssm_state.shape, f32),
            jax.ShapeDtypeStruct((2 * CAPACITY * nt, hid), bf16),
        ),
        in_specs=[pl.BlockSpec(memory_space=V)] * len(operands),
        out_specs=[pl.BlockSpec(memory_space=V)] * 4,
        scratch_shapes=scratch_shapes,
        compiler_params=pltpu.CompilerParams(has_side_effects=True, vmem_limit_bytes=60 * 1024 * 1024),
        name="step",
    )(*operands)


def solution(mesh, nz=4):
    devices = mesh.devices
    nx, nt = devices.shape[0] // nz, devices.shape[1]
    split = Mesh(devices.reshape(nz, nx, nt), REP_TP)
    return jax.shard_map(
        functools.partial(shards, nz, nx, nt),
        mesh=split,
        in_specs=(
            P(REP_TP, None),
            P(None, REP, "tp"),
            P(REP, None, "tp"),
            P(None, REP_TP),
            P(None, REP_TP),
            P(None, REP_TP),
            P(REP_TP),
            P(None, REP_TP),
            P(REP_TP, None, None),
            P("tp", REP),
            P(REP_TP, None),
            P(None, REP_TP),
            P(REP_TP, None),
            P(REP_TP, None, None, None),
            P(REP_TP, None),
        ),
        out_specs=(P(REP_TP, None), P(None, REP, "tp"), P(REP, None, "tp"), P(REP, "tp")),
        check_vma=False,
    )
```

time: 1980 us -> 184 us (0.09)
  blocking collectives: 1490 us -> 0 us
  local copies, waits for them, and re-layouts: 252 us -> 13.1 us
  Pallas kernels: 0 us -> 166 us
  waiting for transfers between devices: 76.8 us -> 0 us
  other arithmetic: 70.1 us -> 2.4 us
  starting transfers between devices: 51.4 us -> 0 us
    all_gather x5 -> x0, blocking collectives: 1380 us -> none  [the longest x1 344 us: shards(): lax.all_gather(decay_log, REP_TP, axis=1, tiled=True)]
    pallas_call x0 -> x1, Pallas kernels: none -> 166 us  [shards(): pl.pallas_call(functools.partial(kernel, nz, nx, nt), out_shape=(jax.Shap...]
    all_to_all x6 -> x0, local copies, waits for them, and re-layouts: 102 us -> none  [the longest x1 62 us: shards(): lax.all_to_all(step_proj.reshape(step_proj.shape[0], 1, 1, inner_all), 't...]
    unnamed x1 -> x0, blocking collectives: 91.6 us -> none
    unnamed x48 -> x10, local copies, waits for them, and re-layouts: 91.4 us -> 8.89 us
    reduce_scatter x2 -> x0, waiting for transfers between devices: 71.6 us -> none  [own_block(): blocks = lax.psum_scatter(blocks, axes[k], scatter_dimension=0, tiled=True)]
    unnamed x3 -> x0, other arithmetic: 62.6 us -> none
    all_to_all x7 -> x0, starting transfers between devices: 50.8 us -> none  [the longest x1 25 us: shards(): lax.all_to_all(replica_rows, REP, split_axis=1, concat_axis=0, tiled=True)]
  transfers between devices with their start and end apart: 11 -> 0, of which waited for: 3 -> 0; matrix products, arithmetic and copies ran while one was open for 11% -> 0% of each run, Pallas kernels for 0% -> 0%
where the time goes in v1:
time: 184 us; the launch traced here: 183 us
  Pallas kernels  166 us (90%)
  local copies, waits for them, and re-layouts  13.1 us (7%)
  other arithmetic  2.4 us (1%)
    pallas_call x1, Pallas kernels, shards(): pl.pallas_call(functools.partial(kernel, nz, nx, nt), out_shape=(jax.Shap...  166 us
    unnamed x10, local copies, waits for them, and re-layouts  8.89 us

profile of v1, /device:TPU:2, one launch (start us, length us, event | category | flops | bytes accessed | tf_op | source)
XLA Modules:
  0.0 182.5 jit_solution(6996544320866553464)
XLA Ops:
  0.7 1.0 slice_reduce_fusion.1
  1.6 0.1 or_convert_fusion
  1.7 0.1 compare_select_fusion
  1.8 0.8 add_convert_fusion
  2.6 0.6 pad.19.info
  3.1 0.7 copy.23
  3.9 1.4 fusion.2.router_gain
  5.2 0.8 copy.19
  6.0 0.8 copy.20
  6.8 0.8 copy.21
  7.5 0.8 copy.22
  8.3 0.1 maximum_bitcast_fusion
  8.4 0.6 pad.17.packed
  9.0 1.4 pad.16.select_t
  10.3 166.3 %step.1 = (bf16[2,4096]{1,0:T(2,128)(2,1)}, bf16[3,32,512]{2,1,0:T(8,128)(2,1)}, f32[32,16,512]{2,1,0:T(8,128)}, bf16[64,768]{1,0:T(8,128)(2,1)}) custom-call(bf16[2,4096]{1,0:T(2,128)(2,1)} %tokens.1, bf16[3,32,512]{2,1,0:T(8,128)(2,1)} %conv_state.1, f32[32,16,512]{2,1,0:T(8,128)} %ssm_state.1, bf16[16,2,8192]{2,1,0:T(2,128)(2,1)} %input_proj.1, ...), custom_call_target="tpu_custom_call" | custom-call | tf_op jit(solution)/shard_map/step/pallas_call | solution.py:376
  176.7 0.0 copy-start
  176.7 1.4 copy.28
  178.0 1.5 copy.29
  179.6 2.3 %copy.30 = f32[32,16,512]{2,1,0:T(8,128)} copy(f32[32,16,512]{2,1,0:T(8,128)} %get-tuple-element.12) | data formatting | bytes 2097152
  181.9 0.0 copy-done
  181.9 0.6 copy.31
  (3 shorter events, 0.0 us)
Async XLA Ops:
  176.7 5.2 %copy-start = (bf16[64,768]{1,0:T(8,128)(2,1)S(1)}, bf16[64,768]{1,0:T(8,128)(2,1)}, u32[]{:S(2)}) copy-start(bf16[64,768]{1,0:T(8,128)(2,1)} %get-tuple-element.13) | copy-start | bytes 294916

commit v2 on v1

v2 whole, which is shorter than its diff:
```python
import functools

import jax
import jax.numpy as jnp
from jax import lax
from jax.experimental import pallas as pl
from jax.experimental.pallas import tpu as pltpu
from jax.sharding import Mesh
from jax.sharding import PartitionSpec as P

CAPACITY = 2
REP = ("rep_0", "rep_1")
REP_TP = ("rep_0", "rep_1", "tp")
MESH = pl.DeviceIdType.MESH
EPS = 1e-05
bf16 = jnp.bfloat16
f32 = jnp.float32
LANES = 128

PHASES = (
    "x1", "xb", "rs", "wi", "gn", "rg", "prz", "sez", "x2", "st",
    "wo", "we0", "we1", "stz", "p3x", "p3z", "prx", "sex", "pr2", "stx",
    "gnx", "rgx", "wox", "wex", "sel", "gz", "mc", "y2", "yo", "info",
    "lz", "yx1", "yx2", "yx3", "ez0", "ez1", "ez2", "ez3", "fin",
)
PH = {name: k for k, name in enumerate(PHASES)}


def sigmoid(v):
    return 1.0 / (1.0 + jnp.exp(-v))


def silu(v):
    return v / (1.0 + jnp.exp(-v))


def softplus(v):
    return jnp.maximum(v, 0.0) + jnp.log1p(jnp.exp(-jnp.abs(v)))


def dot(a, b):
    return jnp.dot(a, b, preferred_element_type=f32)


def dot_nt(a, b):
    return lax.dot_general(a, b, (((1,), (1,)), ((), ())), preferred_element_type=f32)


def kernel(
    nz, nx, nt,
    tokens, conv_state, ssm_state, norm_gains, conv_weight, conv_skip, step_bias, decay_log,
    input_proj, select_t, step_row, output_t, router, expert_proj, expert_ids,
    mamba_out, conv_next, ssm_next, expert_hidden,
    x1, xb, x2, xx, rs_s, rs_r, wi_s, wi_r, gn_s, gn_r, gn_b, gn_x, rg_s, rg_r, rg_x, wo_r, wo_x,
    st_s, st_r, st_b, st_z, st_x, pk, pr_s, pr_z, pr_x, pr2, se_s, se_z, se_x, p3, p3x, p3zs, p3z,
    we_s, we_r, we_x, sel_s, sel_r, maps, step_b, act_b, ro_b, ga_s, g_z,
    mo_s, mc_r, y_s, y2, yo, yx, info_s, info_r, lg, lgz, pe, pez, fin_s, fin,
    ssem, rsem,
):
    nr = nz * nx
    z, x, t = lax.axis_index("rep_0"), lax.axis_index("rep_1"), lax.axis_index("tp")
    r = z * nx + x
    rows = input_proj.shape[0]
    fb = rows * nt
    fz = fb * nx
    ch = ssm_state.shape[2]
    st = ssm_state.shape[1]
    td = tokens.shape[0]
    rq = td * nt
    rank = nr * nt
    hid = expert_proj.shape[3] // nt
    cdev = conv_weight.shape[1]
    per_x = 4 // nx
    groups = {
        "tp": (nt, t, lambda p: {"tp": p}),
        "rep": (nr, r, lambda p: {"rep_0": p // nx, "rep_1": p % nx}),
        "x": (nx, x, lambda p: {"rep_1": p}),
        "z": (nz, z, lambda p: {"rep_0": p}),
    }
    pending = []

    def remote(src, dst, k, device):
        pltpu.make_async_remote_copy(
            src_ref=src, dst_ref=dst, send_sem=ssem.at[k], recv_sem=rsem.at[k],
            device_id=device, device_id_type=MESH,
        ).start()

    def send(group, name, src, dst, at=None, part=None):
        n, me, dev = groups[group]
        k = PH[name]
        at = at or (lambda me: dst.at[me])

        def body(step, carry):
            peer = (me + step) % n
            remote(src(peer), at(me), k, dev(peer))
            return carry

        if n > 1:
            lax.fori_loop(1, n, body, 0)
            pending.append((k, dst.at[pl.ds(0, n - 1)] if part is None else part))
        pltpu.make_async_copy(src(me), at(me), rsem.at[k]).start()

    def arrived(name, dst):
        pltpu.make_async_copy(dst, dst, rsem.at[PH[name]]).wait()

    def cols(ref, p, width):
        return ref.at[:, pl.ds(pl.multiple_of(p * width, width), width)]

    def total(ref):
        acc = ref[0].astype(f32)
        for k in range(1, ref.shape[0]):
            acc = acc + ref[k].astype(f32)
        return acc

    barrier = pltpu.get_barrier_semaphore()
    for group in ("tp", "rep"):
        n, me, dev = groups[group]

        def greet(step, carry, n=n, me=me, dev=dev):
            pl.semaphore_signal(barrier, inc=1, device_id=dev((me + step) % n), device_id_type=MESH)
            return carry

        lax.fori_loop(1, n, greet, 0)

    for j in range(2):
        wi_s[j * rows : (j + 1) * rows, :] = input_proj[:, j, :]
    xf = tokens[...].astype(f32)
    rs = lax.rsqrt(jnp.mean(xf * xf, axis=1, keepdims=True) + EPS)
    rs_s[...] = jnp.broadcast_to(rs, (td, LANES))
    pl.semaphore_wait(barrier, nt - 1 + nr - 1)

    send("rep", "x1", lambda p: cols(tokens, p, fb), x1)
    send("tp", "wi", lambda p: cols(wi_s, p, ch), wi_r)
    gn_s[...] = jnp.zeros(gn_s.shape, bf16)
    gn_s[:, 0:rows] = norm_gains[...]
    send("tp", "gn", lambda p: gn_s, gn_r)
    send("tp", "rs", lambda p: rs_s, rs_r)
    at_row = lax.broadcasted_iota(jnp.int32, (nt, 1), 0) == t
    st_s[...] = jnp.where(at_row, step_row[...].astype(f32), 0.0).astype(bf16)
    pk[...] = jnp.zeros(pk.shape, f32)
    pk[0:4, 0:cdev] = conv_weight[...].astype(f32)
    pk[4:6, 0:cdev] = conv_skip[...].astype(f32)
    pk[6:7, 0:cdev] = step_bias[...].astype(f32)
    pk[7 : 7 + st, 0:cdev] = decay_log[...].astype(f32)
    pr_s[...] = pk[...].astype(bf16)
    se_s[...] = jnp.zeros(se_s.shape, bf16)
    se_s[0 : select_t.shape[0], :] = select_t[...]
    rg_s[...] = jnp.zeros(rg_s.shape, bf16)
    rg_s[:, 0 : router.shape[1]] = router[...]
    arrived("x1", x1)
    send("tp", "x2", lambda p: x1, x2)
    send("tp", "st", lambda p: cols(st_s, p, ch), st_r)
    send("z", "prz", lambda p: pr_s, pr_z)
    send("z", "sez", lambda p: se_s, se_z)
    send("z", "xb", lambda p: cols(tokens, p, fz), xb)
    send("tp", "rg", lambda p: rg_s, rg_r)
    send("tp", "wo", lambda p: cols(output_t, p, ch), wo_r)

    def send_experts(e):
        for j in range(2):
            we_s[2 * e + j] = expert_proj[:, e, j, :]
        half = we_r.at[pl.ds(2 * e, 2)]
        send(
            "tp", "we%d" % e,
            lambda p: we_s.at[pl.ds(2 * e, 2), :, pl.ds(pl.multiple_of(p * hid, hid), hid)], half,
            at=lambda me: half.at[:, me], part=half.at[:, pl.ds(0, nt - 1)],
        )

    send_experts(0)

    arrived("gn", gn_r)
    gnv = gn_r[...].astype(f32)
    gains = jnp.concatenate([gnv[k][:, 0:rows] for k in range(nt)], axis=1)
    gn_b[...] = gains.astype(bf16)
    gain0 = gains[0:1, :]
    arrived("x2", x2)

    def place_in(q, carry):
        block = x2[:, q].reshape(rq, fb).astype(f32)
        xx[q % nx, q // nx] = (block * gain0).astype(bf16)
        return carry

    lax.fori_loop(0, nr, place_in, 0)
    arrived("wi", wi_r)
    lhs = xx[...].reshape(nr * rq, fb)
    for j in range(2):
        w = wi_r[:, j * rows : (j + 1) * rows, :].reshape(fb, ch)
        p3[:, :, :, j * ch : (j + 1) * ch] = dot(lhs, w).astype(bf16).reshape(nx, nz, rq, ch)
    send("x", "p3x", lambda p: p3.at[p], p3x)

    arrived("st", st_r)
    st_b[...] = jnp.sum(st_r[...].astype(f32), axis=0).astype(bf16)
    send("z", "stz", lambda p: st_b, st_z)
    arrived("prz", pr_z)
    send("x", "prx", lambda p: pr_z, pr_x)
    arrived("sez", se_z)
    send("x", "sex", lambda p: se_z, se_x)
    send("x", "gnx", lambda p: gn_b, gn_x)
    arrived("rg", rg_r)
    send("x", "rgx", lambda p: rg_r, rg_x)
    arrived("wo", wo_r)
    send("x", "wox", lambda p: wo_r, wo_x)

    arrived("p3x", p3x)
    p3zs[...] = total(p3x).astype(bf16)
    send("z", "p3z", lambda p: p3zs.at[p], p3z)
    arrived("prx", pr_x)
    send("tp", "pr2", lambda p: pr_x.at[p % nx, p // nx], pr2)
    arrived("stz", st_z)
    send("x", "stx", lambda p: st_z, st_x)
    send_experts(1)
    arrived("sex", se_x)
    srw = se_s.shape[0]
    sp = sel_s.shape[1]
    width = select_t.shape[0]
    shape = (sp, nr * srw)
    at_col = lax.broadcasted_iota(jnp.int32, shape, 0)
    place_of = lax.broadcasted_iota(jnp.int32, shape, 1)
    blk, off = place_of // srw, place_of % srw
    true_col = ((blk % nz) * nx + blk // nz) * width + off
    perm = jnp.where((true_col == at_col) & (off < width), 1.0, 0.0).astype(bf16)
    select_all = dot(perm, se_x[...].reshape(nr * srw, ch)).astype(bf16)
    arrived("rs", rs_r)
    rsv = rs_r[...].reshape(rq, LANES)[:, 0:1]
    arrived("pr2", pr2)
    prv = pr2[...].astype(f32)
    par = jnp.concatenate([prv[k][:, 0:cdev] for k in range(nt)], axis=1)
    history = jnp.sum(par[0:3][:, None, :] * conv_state[...].astype(f32), axis=0) + par[4:5]
    decay_rate = -jnp.exp(par[7 : 7 + st])
    conv_next[0] = conv_state[1]
    conv_next[1] = conv_state[2]
    arrived("p3z", p3z)
    projected = total(p3z) * rsv
    conv_input = projected[:, :ch]
    gate_z = projected[:, ch:]
    conv_next[2] = conv_input.astype(bf16)
    activated = silu(history + par[3:4] * conv_input)
    sel_s[...] = dot_nt(activated.astype(bf16), select_all).astype(bf16)
    send("tp", "sel", lambda p: sel_s, sel_r)
    act_b[...] = activated
    for e in range(2):
        arrived("we%d" % e, we_r.at[pl.ds(2 * e, 2)])
    send("x", "wex", lambda p: we_r.at[pl.ds(p * per_x, per_x)], we_x)
    arrived("stx", st_x)
    step_all = jnp.concatenate([st_x[q % nx, q // nx] for q in range(nr)], axis=0)
    arrived("sel", sel_r)
    selected = total(sel_r)
    step_low = selected[:, :rank].astype(bf16)
    maps[...] = jnp.broadcast_to(selected[:, rank : rank + 2 * st][:, :, None], maps.shape)
    step_b[...] = softplus(dot(step_low, step_all) + par[6:7])

    def token(i, carry):
        s = step_b[pl.ds(i, 1), :]
        a = act_b[pl.ds(i, 1), :]
        m = maps[i]
        wide = jnp.concatenate([m] * (ch // LANES), axis=1)
        nxt = jnp.exp(s * decay_rate) * ssm_state[i] + (s * a) * wide[:st]
        ssm_next[i] = nxt
        ro_b[pl.ds(i, 1), :] = jnp.sum(nxt * wide[st:], axis=0, keepdims=True)
        return carry

    lax.fori_loop(0, rq, token, 0)
    readout = ro_b[...] + par[5:6] * activated
    ga_s[...] = (readout * silu(gate_z)).astype(bf16)

    send("z", "gz", lambda p: ga_s, g_z)
    arrived("wox", wo_x)
    arrived("gz", g_z)
    mo = dot_nt(g_z[...].reshape(nz * rq, ch), wo_x[...].reshape(fz, ch))
    mo_s[...] = mo.astype(bf16).reshape(nz, nt, td, fz)
    send("tp", "mc", lambda p: mo_s.at[:, p], mc_r)
    arrived("xb", xb)
    arrived("mc", mc_r)
    y_s[...] = (xb[...].astype(f32) + total(mc_r)).astype(bf16)
    send("tp", "y2", lambda p: y_s, y2)
    send("z", "yo", lambda p: y_s.at[p], yo)

    arrived("gnx", gn_x)
    gain1 = jnp.concatenate([gn_x[k].astype(f32)[1:2, :] for k in range(nx)], axis=1)
    arrived("rgx", rg_x)
    arrived("y2", y2)
    for q in range(nz):
        block = y2[:, q].reshape(rq, fz).astype(f32)
        yx[0, q] = (block * gain1).astype(bf16)
    for k in range(1, nx):
        remote(yx.at[0], yx.at[k], PH["yx%d" % k], {"rep_1": (x + k) % nx})
        pending.append((PH["yx%d" % k], yx.at[0]))
    arrived("wex", we_x)
    for k in range(nx):
        if k:
            arrived("yx%d" % k, yx.at[k])
        left = yx[k].reshape(nz * rq, fz)
        for c in range(per_x):
            part = dot(left, we_x[:, c].reshape(fz, hid))
            pe[k, :, c] = part.astype(bf16).reshape(nz, rq, hid)
        send("z", "ez%d" % k, lambda p, k=k: pe.at[k, p], pez.at[k])
        if k == 0:
            lg[...] = dot(left, rg_x[...].reshape(fz, LANES)).astype(bf16).reshape(nz, rq, LANES)
            send("z", "lz", lambda p: lg.at[p], lgz)

    arrived("yo", yo)
    yov = [yo[k].astype(f32) for k in range(nz)]
    square = jnp.zeros((td, 1), f32)
    for k in range(nz):
        mamba_out[:, k * fz : (k + 1) * fz] = yo[k]
        square = square + jnp.sum(yov[k] * yov[k], axis=1, keepdims=True)
    rs2 = lax.rsqrt(square * (1.0 / (nr * fb)) + EPS)
    lane = lax.broadcasted_iota(jnp.int32, (td, LANES), 1)
    ids = expert_ids[...].astype(f32)
    ida, idb = ids[:, 0:1], ids[:, 1:2]
    about = jnp.where(lane == 0, rs2, jnp.where(lane == 1, ida, idb))
    for e in range(2):
        names = jnp.where((ida == e) | (idb == e), 1.0, 0.0)
        before = [jnp.zeros((1, 1), f32)]
        for k in range(1, td):
            before.append(before[-1] + names[k - 1 : k, :])
        want = jnp.where(names > 0.0, e * CAPACITY + jnp.concatenate(before, axis=0), -1.0)
        about = jnp.where(lane == 3 + e, want, about)
    info_s[...] = about
    send("tp", "info", lambda p: info_s, info_r)

    for k in range(nx):
        arrived("ez%d" % k, pez.at[k])
        done = total(pez.at[k]).astype(bf16)
        if k == 0:
            fin[pl.ds(x, 1)] = done[None]
        else:
            fin_s[k] = done
            remote(fin_s.at[k], fin.at[x], PH["fin"], {"rep_1": (x + nx - k) % nx})

    arrived("info", info_r)
    arrived("lz", lgz)
    inf = info_r[...].reshape(rq, LANES)
    scale = inf[:, 0:1]
    id0, id1 = inf[:, 1:2], inf[:, 2:3]
    logits = total(lgz) * scale
    lane = lax.broadcasted_iota(jnp.int32, (rq, LANES), 1).astype(f32)
    zero = jnp.zeros((), f32)
    first = jnp.sum(jnp.where(lane == id0, logits, zero), axis=1, keepdims=True)
    second = jnp.sum(jnp.where(lane == id1, logits, zero), axis=1, keepdims=True)
    gate_first = sigmoid(first - second)
    gate_second = sigmoid(second - first)
    inft = inf.T
    slots = 2 * CAPACITY * nt
    slot = lax.broadcasted_iota(jnp.int32, (slots, rq), 0).astype(f32)
    token_at = lax.broadcasted_iota(jnp.int32, (slots, rq), 1)
    base = ((token_at // td) * (2 * CAPACITY)).astype(f32)
    others = fin.at[pl.ds(0, nx - 1)]
    if nx > 1:
        arrived("fin", others)
        pending.append((PH["fin"], others))
    result = jnp.zeros((slots, hid), f32)
    for e in range(2):
        gate = jnp.where(id0 == e, gate_first, zero) + jnp.where(id1 == e, gate_second, zero)
        gate = gate.astype(bf16).astype(f32)
        halves = []
        for j in range(2):
            q = 2 * e + j
            halves.append(fin[q // per_x, q % per_x].astype(f32) * scale)
        hidden = (gate * silu(halves[0]) * halves[1]).astype(bf16)
        want = inft[3 + e : 4 + e, :]
        pick = jnp.where((slot == base + want) & (want >= 0.0), 1.0, 0.0).astype(bf16)
        result = result + dot(pick, hidden)
    expert_hidden[...] = result.astype(bf16)

    for k, part in pending:
        pltpu.make_async_copy(part, part, ssem.at[k]).wait()


def shards(
    nz, nx, nt, tokens, conv_state, ssm_state, norm_gains, conv_weight, conv_skip, step_bias, decay_log,
    input_proj, select_proj, step_proj, output_proj, router, expert_proj, expert_ids,
):
    nr = nz * nx
    rows = input_proj.shape[0]
    td, model = tokens.shape
    rq = td * nt
    fb = rows * nt
    fz = fb * nx
    _, st, ch = ssm_state.shape
    hid = expert_proj.shape[3] // nt
    width = select_proj.shape[1]
    srw = -(-width // 8) * 8
    sp = -(-width * nr // LANES) * LANES
    prw = -(-(7 + st) // 8) * 8
    per_x = 4 // nx
    oc = output_proj.shape[1]

    V = pltpu.VMEM
    scratch = dict(
        x1=((nr, td, fb), bf16), xb=((nz, td, fz), bf16), x2=((nt, nr, td, fb), bf16),
        xx=((nx, nz, rq, fb), bf16),
        rs_s=((td, LANES), f32), rs_r=((nt, td, LANES), f32),
        wi_s=((2 * rows, nt * ch), bf16), wi_r=((nt, 2 * rows, ch), bf16),
        gn_s=((2, LANES), bf16), gn_r=((nt, 2, LANES), bf16), gn_b=((2, fb), bf16), gn_x=((nx, 2, fb), bf16),
        rg_s=((rows, LANES), bf16), rg_r=((nt, rows, LANES), bf16), rg_x=((nx, nt, rows, LANES), bf16),
        wo_r=((nt, oc, ch), bf16), wo_x=((nx, nt, oc, ch), bf16),
        st_s=((nt, nt * ch), bf16), st_r=((nt, nt, ch), bf16), st_b=((nt, ch), bf16),
        st_z=((nz, nt, ch), bf16), st_x=((nx, nz, nt, ch), bf16),
        pk=((prw, LANES), f32), pr_s=((prw, LANES), bf16), pr_z=((nz, prw, LANES), bf16),
        pr_x=((nx, nz, prw, LANES), bf16), pr2=((nt, prw, LANES), bf16),
        se_s=((srw, ch), bf16), se_z=((nz, srw, ch), bf16), se_x=((nx, nz, srw, ch), bf16),
        p3=((nx, nz, rq, 2 * ch), bf16), p3x=((nx, nz, rq, 2 * ch), bf16),
        p3zs=((nz, rq, 2 * ch), bf16), p3z=((nz, rq, 2 * ch), bf16),
        we_s=((4, rows, nt * hid), bf16), we_r=((4, nt, rows, hid), bf16), we_x=((nx, per_x, nt, rows, hid), bf16),
        sel_s=((rq, sp), bf16), sel_r=((nt, rq, sp), bf16),
        maps=((rq, 2 * st, LANES), f32), step_b=((rq, ch), f32), act_b=((rq, ch), f32),
        ro_b=((rq, ch), f32),
        ga_s=((rq, ch), bf16), g_z=((nz, rq, ch), bf16),
        mo_s=((nz, nt, td, fz), bf16), mc_r=((nt, nz, td, fz), bf16), y_s=((nz, td, fz), bf16),
        y2=((nt, nz, td, fz), bf16), yo=((nz, td, fz), bf16), yx=((nx, nz, rq, fz), bf16),
        info_s=((td, LANES), f32), info_r=((nt, td, LANES), f32),
        lg=((nz, rq, LANES), bf16), lgz=((nz, rq, LANES), bf16),
        pe=((nx, nz, per_x, rq, hid), bf16), pez=((nx, nz, per_x, rq, hid), bf16),
        fin_s=((nx, per_x, rq, hid), bf16), fin=((nx, per_x, rq, hid), bf16),
    )
    scratch_shapes = [V(s, d) for s, d in scratch.values()]
    scratch_shapes += [pltpu.SemaphoreType.DMA((len(PHASES),))] * 2
    operands = (
        tokens, conv_state, ssm_state, norm_gains, conv_weight, conv_skip, step_bias[None], decay_log,
        input_proj, select_proj.T, step_proj, output_proj.T, router, expert_proj, expert_ids,
    )
    return pl.pallas_call(
        functools.partial(kernel, nz, nx, nt),
        out_shape=(
            jax.ShapeDtypeStruct((td, model), bf16),
            jax.ShapeDtypeStruct(conv_state.shape, bf16),
            jax.ShapeDtypeStruct(ssm_state.shape, f32),
            jax.ShapeDtypeStruct((2 * CAPACITY * nt, hid), bf16),
        ),
        in_specs=[pl.BlockSpec(memory_space=V)] * len(operands),
        out_specs=[pl.BlockSpec(memory_space=V)] * 4,
        scratch_shapes=scratch_shapes,
        compiler_params=pltpu.CompilerParams(
            collective_id=0, has_side_effects=True, vmem_limit_bytes=60 * 1024 * 1024
        ),
        name="step",
    )(*operands)


def solution(mesh, nz=4):
    devices = mesh.devices
    nx, nt = devices.shape[0] // nz, devices.shape[1]
    split = Mesh(devices.reshape(nz, nx, nt), REP_TP)
    return jax.shard_map(
        functools.partial(shards, nz, nx, nt),
        mesh=split,
        in_specs=(
            P(REP_TP, None),
            P(None, REP, "tp"),
            P(REP, None, "tp"),
            P(None, REP_TP),
            P(None, REP_TP),
            P(None, REP_TP),
            P(REP_TP),
            P(None, REP_TP),
            P(REP_TP, None, None),
            P("tp", REP),
            P(REP_TP, None),
            P(None, REP_TP),
            P(REP_TP, None),
            P(REP_TP, None, None, None),
            P(REP_TP, None),
        ),
        out_specs=(P(REP_TP, None), P(None, REP, "tp"), P(REP, None, "tp"), P(REP, "tp")),
        check_vma=False,
    )
```

time: 184 us -> 129 us (0.70)
  Pallas kernels: 166 us -> 122 us
  local copies, waits for them, and re-layouts: 13.1 us -> 5.86 us
  other arithmetic: 2.4 us -> 0 us
    pallas_call x1, Pallas kernels: 166 us -> 122 us  [shards(): pl.pallas_call(functools.partial(kernel, nz, nx, nt), out_shape=(jax.Shap...]
    unnamed x10 -> x6, local copies, waits for them, and re-layouts: 8.89 us -> 5.86 us
    pad x3 -> x0, local copies, waits for them, and re-layouts: 2.54 us -> none  [the longest x1 1.36 us: shards(): select_t = jnp.pad(select_t, ((0, srw - select_t.shape[0]), (0, 0)))]
where the time goes in v2:
time: 129 us
  Pallas kernels  122 us (95%)
  local copies, waits for them, and re-layouts  5.86 us (5%)
    pallas_call x1, Pallas kernels, shards(): pl.pallas_call(functools.partial(kernel, nz, nx, nt), out_shape=(jax.Shap...  122 us
    unnamed x6, local copies, waits for them, and re-layouts  5.86 us

profile of v2, /device:TPU:2, one launch (start us, length us, event | category | flops | bytes accessed | tf_op | source)
XLA Modules:
  0.0 128.8 jit_solution(13691001419787935910)
XLA Ops:
  0.6 122.3 %step.1 = (bf16[2,4096]{1,0:T(2,128)(2,1)}, bf16[3,32,512]{2,1,0:T(8,128)(2,1)}, f32[32,16,512]{2,1,0:T(8,128)}, bf16[64,768]{1,0:T(8,128)(2,1)}) custom-call(bf16[2,4096]{1,0:T(2,128)(2,1)} %tokens.1, bf16[3,32,512]{2,1,0:T(8,128)(2,1)} %conv_state.1, f32[32,16,512]{2,1,0:T(8,128)} %ssm_state.1, bf16[2,16]{1,0:T(2,128)(2,1)} %norm_gains.1, ...), custom_call_target="tpu_custom_call" | custom-call | tf_op jit(solution)/shard_map/step/pallas_call | solution.py:423
  122.9 0.0 copy-start
  122.9 1.4 %copy.23 = bf16[2,4096]{1,0:T(2,128)(2,1)} copy(bf16[2,4096]{1,0:T(2,128)(2,1)} %get-tuple-element.8) | data formatting | bytes 32768
  124.3 1.5 %copy.24 = bf16[3,32,512]{2,1,0:T(8,128)(2,1)} copy(bf16[3,32,512]{2,1,0:T(8,128)(2,1)} %get-tuple-element.9) | data formatting | bytes 196608
  125.8 2.3 %copy.25 = f32[32,16,512]{2,1,0:T(8,128)} copy(f32[32,16,512]{2,1,0:T(8,128)} %get-tuple-element.10) | data formatting | bytes 2097152
  128.1 0.0 copy-done
  128.1 0.6 copy.26
Async XLA Ops:
  122.9 5.2 %copy-start = (bf16[64,768]{1,0:T(8,128)(2,1)S(1)}, bf16[64,768]{1,0:T(8,128)(2,1)}, u32[]{:S(2)}) copy-start(bf16[64,768]{1,0:T(8,128)(2,1)} %get-tuple-element.11) | copy-start | bytes 294916

commit v3 on v2

--- a/solution.py
+++ b/solution.py
@@ -18,10 +18,11 @@
 LANES = 128
 
 PHASES = (
-    "x1", "xb", "rs", "wi", "gn", "rg", "prz", "sez", "x2", "st",
-    "wo", "we0", "we1", "stz", "p3x", "p3z", "prx", "sex", "pr2", "stx",
-    "gnx", "rgx", "wox", "wex", "sel", "gz", "mc", "y2", "yo", "info",
-    "lz", "yx1", "yx2", "yx3", "ez0", "ez1", "ez2", "ez3", "fin",
+    "x1", "xb", "rs", "wi0", "wi1", "gn", "rg", "prz", "sez", "x2",
+    "st", "wo", "we0", "we1", "stz", "p3x0", "p3x1", "p3z0", "p3z1", "prx",
+    "sex", "pr2", "stx", "gnx", "rgx", "wox", "wex", "sel", "gz", "mc",
+    "y2", "yo", "info", "lz", "ysx", "y2b", "yx1", "yx2", "yx3", "ez0",
+    "ez1", "ez2", "ez3", "fin",
 )
 PH = {name: k for k, name in enumerate(PHASES)}
 
@@ -46,16 +47,25 @@
     return lax.dot_general(a, b, (((1,), (1,)), ((), ())), preferred_element_type=f32)
 
 
+def write_out(*refs):
+    copies = [pltpu.make_async_copy(refs[k], refs[4 + k], refs[8].at[k]) for k in range(4)]
+    for copy in copies:
+        copy.start()
+    for copy in copies:
+        copy.wait()
+
+
 def kernel(
     nz, nx, nt,
-    tokens, conv_state, ssm_state, norm_gains, conv_weight, conv_skip, step_bias, decay_log,
-    input_proj, select_t, step_row, output_t, router, expert_proj, expert_ids,
+    tokens, norm_gains, conv_weight, conv_skip, step_bias, decay_log, step_row, router, expert_ids,
+    input_hbm, select_hbm, output_hbm, expert_hbm, conv_hbm, ssm_hbm,
     mamba_out, conv_next, ssm_next, expert_hidden,
-    x1, xb, x2, xx, rs_s, rs_r, wi_s, wi_r, gn_s, gn_r, gn_b, gn_x, rg_s, rg_r, rg_x, wo_r, wo_x,
+    input_proj, select_t, output_t, expert_proj, conv_state, ssm_state,
+    x1, xb, x2, xx, rs_s, rs_r, wi_s, wi_r, gn_s, gn_r, gn_b, gn_x, rg_s, rg_r, rg_b, rg_x, wo_r, wo_x,
     st_s, st_r, st_b, st_z, st_x, pk, pr_s, pr_z, pr_x, pr2, se_s, se_z, se_x, p3, p3x, p3zs, p3z,
     we_s, we_r, we_x, sel_s, sel_r, maps, step_b, act_b, ro_b, ga_s, g_z,
-    mo_s, mc_r, y_s, y2, yo, yx, info_s, info_r, lg, lgz, pe, pez, fin_s, fin,
-    ssem, rsem,
+    mo_s, mc_r, y_s, y2, ysx, y2b, yo, yx, info_s, info_r, lg, lgz, pe, pez, fin_s, fin,
+    ssem, rsem, lsem,
 ):
     nr = nz * nx
     z, x, t = lax.axis_index("rep_0"), lax.axis_index("rep_1"), lax.axis_index("tp")
@@ -122,39 +132,47 @@
 
         lax.fori_loop(1, n, greet, 0)
 
-    for j in range(2):
-        wi_s[j * rows : (j + 1) * rows, :] = input_proj[:, j, :]
-    xf = tokens[...].astype(f32)
-    rs = lax.rsqrt(jnp.mean(xf * xf, axis=1, keepdims=True) + EPS)
-    rs_s[...] = jnp.broadcast_to(rs, (td, LANES))
-    pl.semaphore_wait(barrier, nt - 1 + nr - 1)
-
-    send("rep", "x1", lambda p: cols(tokens, p, fb), x1)
-    send("tp", "wi", lambda p: cols(wi_s, p, ch), wi_r)
+    loads = {}
+    for k, (name, src, dst) in enumerate((
+        ("input", input_hbm, input_proj), ("select", select_hbm, select_t), ("output", output_hbm, output_t),
+        ("expert", expert_hbm, expert_proj), ("conv", conv_hbm, conv_state), ("ssm", ssm_hbm, ssm_state),
+    )):
+        loads[name] = pltpu.make_async_copy(src, dst, lsem.at[k])
+        loads[name].start()
+
     gn_s[...] = jnp.zeros(gn_s.shape, bf16)
     gn_s[:, 0:rows] = norm_gains[...]
+    loads["input"].wait()
+    pl.semaphore_wait(barrier, nt - 1 + nr - 1)
+    send("rep", "x1", lambda p: cols(tokens, p, fb), x1)
     send("tp", "gn", lambda p: gn_s, gn_r)
-    send("tp", "rs", lambda p: rs_s, rs_r)
-    at_row = lax.broadcasted_iota(jnp.int32, (nt, 1), 0) == t
-    st_s[...] = jnp.where(at_row, step_row[...].astype(f32), 0.0).astype(bf16)
+    for j in range(2):
+        wi_s[j] = input_proj[:, j, :]
+        send("tp", "wi%d" % j, lambda p, j=j: cols(wi_s.at[j], p, ch), wi_r.at[j])
     pk[...] = jnp.zeros(pk.shape, f32)
     pk[0:4, 0:cdev] = conv_weight[...].astype(f32)
     pk[4:6, 0:cdev] = conv_skip[...].astype(f32)
     pk[6:7, 0:cdev] = step_bias[...].astype(f32)
     pk[7 : 7 + st, 0:cdev] = decay_log[...].astype(f32)
     pr_s[...] = pk[...].astype(bf16)
+    send("z", "prz", lambda p: pr_s, pr_z)
     se_s[...] = jnp.zeros(se_s.shape, bf16)
+    loads["select"].wait()
     se_s[0 : select_t.shape[0], :] = select_t[...]
-    rg_s[...] = jnp.zeros(rg_s.shape, bf16)
-    rg_s[:, 0 : router.shape[1]] = router[...]
+    send("z", "sez", lambda p: se_s, se_z)
+    send("z", "xb", lambda p: cols(tokens, p, fz), xb)
+    at_row = lax.broadcasted_iota(jnp.int32, (nt, 1), 0) == t
+    st_s[...] = jnp.where(at_row, step_row[...].astype(f32), 0.0).astype(bf16)
     arrived("x1", x1)
     send("tp", "x2", lambda p: x1, x2)
     send("tp", "st", lambda p: cols(st_s, p, ch), st_r)
-    send("z", "prz", lambda p: pr_s, pr_z)
-    send("z", "sez", lambda p: se_s, se_z)
-    send("z", "xb", lambda p: cols(tokens, p, fz), xb)
+    xf = tokens[...].astype(f32)
+    rs = lax.rsqrt(jnp.mean(xf * xf, axis=1, keepdims=True) + EPS)
+    rs_s[...] = jnp.broadcast_to(rs, (td, LANES))
+    send("tp", "rs", lambda p: rs_s, rs_r)
+    rg_s[...] = jnp.zeros(rg_s.shape, bf16)
+    rg_s[:, 0 : router.shape[1]] = router[...]
     send("tp", "rg", lambda p: rg_s, rg_r)
-    send("tp", "wo", lambda p: cols(output_t, p, ch), wo_r)
 
     def send_experts(e):
         for j in range(2):
@@ -166,8 +184,8 @@
             at=lambda me: half.at[:, me], part=half.at[:, pl.ds(0, nt - 1)],
         )
 
-    send_experts(0)
-
+    arrived("prz", pr_z)
+    send("x", "prx", lambda p: pr_z, pr_x)
     arrived("gn", gn_r)
     gnv = gn_r[...].astype(f32)
     gains = jnp.concatenate([gnv[k][:, 0:rows] for k in range(nt)], axis=1)
@@ -181,34 +199,47 @@
         return carry
 
     lax.fori_loop(0, nr, place_in, 0)
-    arrived("wi", wi_r)
     lhs = xx[...].reshape(nr * rq, fb)
-    for j in range(2):
-        w = wi_r[:, j * rows : (j + 1) * rows, :].reshape(fb, ch)
-        p3[:, :, :, j * ch : (j + 1) * ch] = dot(lhs, w).astype(bf16).reshape(nx, nz, rq, ch)
-    send("x", "p3x", lambda p: p3.at[p], p3x)
+
+    def partial_in(j):
+        arrived("wi%d" % j, wi_r.at[j])
+        p3[j] = dot(lhs, wi_r[j].reshape(fb, ch)).astype(bf16).reshape(nx, nz, rq, ch)
+
+    def send_in(j):
+        send("x", "p3x%d" % j, lambda p: p3.at[j, p], p3x.at[j])
+
+    def sum_in(j):
+        arrived("p3x%d" % j, p3x.at[j])
+        p3zs[j] = total(p3x.at[j]).astype(bf16)
+        send("z", "p3z%d" % j, lambda p: p3zs.at[j, p], p3z.at[j])
+
+    partial_in(0)
+    send_in(0)
 
     arrived("st", st_r)
     st_b[...] = jnp.sum(st_r[...].astype(f32), axis=0).astype(bf16)
     send("z", "stz", lambda p: st_b, st_z)
-    arrived("prz", pr_z)
-    send("x", "prx", lambda p: pr_z, pr_x)
     arrived("sez", se_z)
     send("x", "sex", lambda p: se_z, se_x)
+    partial_in(1)
+    arrived("prx", pr_x)
+    send("tp", "pr2", lambda p: pr_x.at[p % nx, p // nx], pr2)
+    loads["output"].wait()
+    send("tp", "wo", lambda p: cols(output_t, p, ch), wo_r)
+    loads["expert"].wait()
+    send_experts(0)
+    arrived("stz", st_z)
+    send("x", "stx", lambda p: st_z, st_x)
+    send_in(1)
+    sum_in(0)
+    send_experts(1)
+    arrived("rg", rg_r)
+    rgt = rg_r[...].reshape(fb, LANES).astype(f32).T
+    rg_b[...] = rgt[0 : rg_b.shape[0]].astype(bf16)
     send("x", "gnx", lambda p: gn_b, gn_x)
-    arrived("rg", rg_r)
-    send("x", "rgx", lambda p: rg_r, rg_x)
+    send("x", "rgx", lambda p: rg_b, rg_x)
     arrived("wo", wo_r)
     send("x", "wox", lambda p: wo_r, wo_x)
-
-    arrived("p3x", p3x)
-    p3zs[...] = total(p3x).astype(bf16)
-    send("z", "p3z", lambda p: p3zs.at[p], p3z)
-    arrived("prx", pr_x)
-    send("tp", "pr2", lambda p: pr_x.at[p % nx, p // nx], pr2)
-    arrived("stz", st_z)
-    send("x", "stx", lambda p: st_z, st_x)
-    send_experts(1)
     arrived("sex", se_x)
     srw = se_s.shape[0]
     sp = sel_s.shape[1]
@@ -225,22 +256,23 @@
     arrived("pr2", pr2)
     prv = pr2[...].astype(f32)
     par = jnp.concatenate([prv[k][:, 0:cdev] for k in range(nt)], axis=1)
+    loads["conv"].wait()
     history = jnp.sum(par[0:3][:, None, :] * conv_state[...].astype(f32), axis=0) + par[4:5]
     decay_rate = -jnp.exp(par[7 : 7 + st])
     conv_next[0] = conv_state[1]
     conv_next[1] = conv_state[2]
-    arrived("p3z", p3z)
-    projected = total(p3z) * rsv
-    conv_input = projected[:, :ch]
-    gate_z = projected[:, ch:]
+    arrived("p3z0", p3z.at[0])
+    conv_input = total(p3z.at[0]) * rsv
     conv_next[2] = conv_input.astype(bf16)
     activated = silu(history + par[3:4] * conv_input)
     sel_s[...] = dot_nt(activated.astype(bf16), select_all).astype(bf16)
     send("tp", "sel", lambda p: sel_s, sel_r)
     act_b[...] = activated
+    sum_in(1)
     for e in range(2):
         arrived("we%d" % e, we_r.at[pl.ds(2 * e, 2)])
     send("x", "wex", lambda p: we_r.at[pl.ds(p * per_x, per_x)], we_x)
+    loads["ssm"].wait()
     arrived("stx", st_x)
     step_all = jnp.concatenate([st_x[q % nx, q // nx] for q in range(nr)], axis=0)
     arrived("sel", sel_r)
@@ -261,6 +293,8 @@
 
     lax.fori_loop(0, rq, token, 0)
     readout = ro_b[...] + par[5:6] * activated
+    arrived("p3z1", p3z.at[1])
+    gate_z = total(p3z.at[1]) * rsv
     ga_s[...] = (readout * silu(gate_z)).astype(bf16)
 
     send("z", "gz", lambda p: ga_s, g_z)
@@ -272,22 +306,40 @@
     arrived("xb", xb)
     arrived("mc", mc_r)
     y_s[...] = (xb[...].astype(f32) + total(mc_r)).astype(bf16)
+    relay = nx // 2 if nx > 2 else 0
+    if relay:
+        remote(y_s, ysx, PH["ysx"], {"rep_1": (x + relay) % nx})
+        pending.append((PH["ysx"], ysx))
     send("tp", "y2", lambda p: y_s, y2)
     send("z", "yo", lambda p: y_s.at[p], yo)
 
     arrived("gnx", gn_x)
     gain1 = jnp.concatenate([gn_x[k].astype(f32)[1:2, :] for k in range(nx)], axis=1)
     arrived("rgx", rg_x)
+    experts = rg_b.shape[0]
+    router_all = jnp.concatenate([rg_x[k] for k in range(nx)], axis=1)
+    if relay:
+        arrived("ysx", ysx)
+        send("tp", "y2b", lambda p: ysx, y2b)
+
+    def place_out(src, k):
+        for q in range(nz):
+            block = src[:, q].reshape(rq, fz).astype(f32)
+            yx[k, q] = (block * gain1).astype(bf16)
+
     arrived("y2", y2)
-    for q in range(nz):
-        block = y2[:, q].reshape(rq, fz).astype(f32)
-        yx[0, q] = (block * gain1).astype(bf16)
+    place_out(y2, 0)
     for k in range(1, nx):
-        remote(yx.at[0], yx.at[k], PH["yx%d" % k], {"rep_1": (x + k) % nx})
-        pending.append((PH["yx%d" % k], yx.at[0]))
+        if k != relay:
+            remote(yx.at[0], yx.at[k], PH["yx%d" % k], {"rep_1": (x + k) % nx})
+            pending.append((PH["yx%d" % k], yx.at[0]))
     arrived("wex", we_x)
-    for k in range(nx):
-        if k:
+    order = [0] + ([relay] if relay else []) + [k for k in range(1, nx) if k != relay]
+    for k in order:
+        if relay and k == relay:
+            arrived("y2b", y2b)
+            place_out(y2b, k)
+        elif k:
             arrived("yx%d" % k, yx.at[k])
         left = yx[k].reshape(nz * rq, fz)
         for c in range(per_x):
@@ -295,7 +347,7 @@
             pe[k, :, c] = part.astype(bf16).reshape(nz, rq, hid)
         send("z", "ez%d" % k, lambda p, k=k: pe.at[k, p], pez.at[k])
         if k == 0:
-            lg[...] = dot(left, rg_x[...].reshape(fz, LANES)).astype(bf16).reshape(nz, rq, LANES)
+            lg[:, :, 0:experts] = dot_nt(left, router_all).astype(bf16).reshape(nz, rq, experts)
             send("z", "lz", lambda p: lg.at[p], lgz)
 
     arrived("yo", yo)
@@ -319,7 +371,7 @@
     info_s[...] = about
     send("tp", "info", lambda p: info_s, info_r)
 
-    for k in range(nx):
+    for k in order:
         arrived("ez%d" % k, pez.at[k])
         done = total(pez.at[k]).astype(bf16)
         if k == 0:
@@ -333,8 +385,8 @@
     inf = info_r[...].reshape(rq, LANES)
     scale = inf[:, 0:1]
     id0, id1 = inf[:, 1:2], inf[:, 2:3]
-    logits = total(lgz) * scale
-    lane = lax.broadcasted_iota(jnp.int32, (rq, LANES), 1).astype(f32)
+    logits = (total(lgz) * scale)[:, 0:experts]
+    lane = lax.broadcasted_iota(jnp.int32, (rq, experts), 1).astype(f32)
     zero = jnp.zeros((), f32)
     first = jnp.sum(jnp.where(lane == id0, logits, zero), axis=1, keepdims=True)
     second = jnp.sum(jnp.where(lane == id1, logits, zero), axis=1, keepdims=True)
@@ -387,55 +439,66 @@
     oc = output_proj.shape[1]
 
     V = pltpu.VMEM
-    scratch = dict(
+    experts = router.shape[1]
+    small = (
+        tokens, norm_gains, conv_weight, conv_skip, step_bias[None], decay_log, step_proj, router, expert_ids,
+    )
+    large = (input_proj, select_proj.T, output_proj.T, expert_proj, conv_state, ssm_state)
+    scratch = {"load%d" % k: (a.shape, a.dtype) for k, a in enumerate(large)}
+    scratch.update(
         x1=((nr, td, fb), bf16), xb=((nz, td, fz), bf16), x2=((nt, nr, td, fb), bf16),
         xx=((nx, nz, rq, fb), bf16),
         rs_s=((td, LANES), f32), rs_r=((nt, td, LANES), f32),
-        wi_s=((2 * rows, nt * ch), bf16), wi_r=((nt, 2 * rows, ch), bf16),
+        wi_s=((2, rows, nt * ch), bf16), wi_r=((2, nt, rows, ch), bf16),
         gn_s=((2, LANES), bf16), gn_r=((nt, 2, LANES), bf16), gn_b=((2, fb), bf16), gn_x=((nx, 2, fb), bf16),
-        rg_s=((rows, LANES), bf16), rg_r=((nt, rows, LANES), bf16), rg_x=((nx, nt, rows, LANES), bf16),
+        rg_s=((rows, LANES), bf16), rg_r=((nt, rows, LANES), bf16), rg_b=((experts, fb), bf16),
+        rg_x=((nx, experts, fb), bf16),
         wo_r=((nt, oc, ch), bf16), wo_x=((nx, nt, oc, ch), bf16),
         st_s=((nt, nt * ch), bf16), st_r=((nt, nt, ch), bf16), st_b=((nt, ch), bf16),
         st_z=((nz, nt, ch), bf16), st_x=((nx, nz, nt, ch), bf16),
         pk=((prw, LANES), f32), pr_s=((prw, LANES), bf16), pr_z=((nz, prw, LANES), bf16),
         pr_x=((nx, nz, prw, LANES), bf16), pr2=((nt, prw, LANES), bf16),
         se_s=((srw, ch), bf16), se_z=((nz, srw, ch), bf16), se_x=((nx, nz, srw, ch), bf16),
-        p3=((nx, nz, rq, 2 * ch), bf16), p3x=((nx, nz, rq, 2 * ch), bf16),
-        p3zs=((nz, rq, 2 * ch), bf16), p3z=((nz, rq, 2 * ch), bf16),
+        p3=((2, nx, nz, rq, ch), bf16), p3x=((2, nx, nz, rq, ch), bf16),
+        p3zs=((2, nz, rq, ch), bf16), p3z=((2, nz, rq, ch), bf16),
         we_s=((4, rows, nt * hid), bf16), we_r=((4, nt, rows, hid), bf16), we_x=((nx, per_x, nt, rows, hid), bf16),
         sel_s=((rq, sp), bf16), sel_r=((nt, rq, sp), bf16),
         maps=((rq, 2 * st, LANES), f32), step_b=((rq, ch), f32), act_b=((rq, ch), f32),
         ro_b=((rq, ch), f32),
         ga_s=((rq, ch), bf16), g_z=((nz, rq, ch), bf16),
         mo_s=((nz, nt, td, fz), bf16), mc_r=((nt, nz, td, fz), bf16), y_s=((nz, td, fz), bf16),
-        y2=((nt, nz, td, fz), bf16), yo=((nz, td, fz), bf16), yx=((nx, nz, rq, fz), bf16),
+        y2=((nt, nz, td, fz), bf16), ysx=((nz, td, fz), bf16), y2b=((nt, nz, td, fz), bf16), yo=((nz, td, fz), bf16), yx=((nx, nz, rq, fz), bf16),
         info_s=((td, LANES), f32), info_r=((nt, td, LANES), f32),
         lg=((nz, rq, LANES), bf16), lgz=((nz, rq, LANES), bf16),
         pe=((nx, nz, per_x, rq, hid), bf16), pez=((nx, nz, per_x, rq, hid), bf16),
         fin_s=((nx, per_x, rq, hid), bf16), fin=((nx, per_x, rq, hid), bf16),
     )
     scratch_shapes = [V(s, d) for s, d in scratch.values()]
-    scratch_shapes += [pltpu.SemaphoreType.DMA((len(PHASES),))] * 2
-    operands = (
-        tokens, conv_state, ssm_state, norm_gains, conv_weight, conv_skip, step_bias[None], decay_log,
-        input_proj, select_proj.T, step_proj, output_proj.T, router, expert_proj, expert_ids,
+    scratch_shapes += [pltpu.SemaphoreType.DMA((len(PHASES),))] * 2 + [pltpu.SemaphoreType.DMA((len(large),))]
+    outs = (
+        ((td, model), bf16), (conv_state.shape, bf16), (ssm_state.shape, f32),
+        ((2 * CAPACITY * nt, hid), bf16),
     )
-    return pl.pallas_call(
+    results = pl.pallas_call(
         functools.partial(kernel, nz, nx, nt),
-        out_shape=(
-            jax.ShapeDtypeStruct((td, model), bf16),
-            jax.ShapeDtypeStruct(conv_state.shape, bf16),
-            jax.ShapeDtypeStruct(ssm_state.shape, f32),
-            jax.ShapeDtypeStruct((2 * CAPACITY * nt, hid), bf16),
-        ),
-        in_specs=[pl.BlockSpec(memory_space=V)] * len(operands),
+        out_shape=tuple(V(s, d) for s, d in outs),
+        in_specs=[pl.BlockSpec(memory_space=V)] * len(small) + [pl.BlockSpec(memory_space=pl.ANY)] * len(large),
         out_specs=[pl.BlockSpec(memory_space=V)] * 4,
         scratch_shapes=scratch_shapes,
         compiler_params=pltpu.CompilerParams(
-            collective_id=0, has_side_effects=True, vmem_limit_bytes=60 * 1024 * 1024
+            collective_id=0, has_side_effects=True, vmem_limit_bytes=61 * 1024 * 1024
         ),
         name="step",
-    )(*operands)
+    )(*small, *large)
+    results = [pltpu.with_memory_space_constraint(a, V) for a in results]
+    return pl.pallas_call(
+        write_out,
+        out_shape=tuple(jax.ShapeDtypeStruct(s, d) for s, d in outs),
+        in_specs=[pl.BlockSpec(memory_space=V)] * 4,
+        out_specs=[pl.BlockSpec(memory_space=pl.ANY)] * 4,
+        scratch_shapes=[pltpu.SemaphoreType.DMA((4,))],
+        name="write_out",
+    )(*results)
 
 
 def solution(mesh, nz=4):

time: 129 us -> 111 us (0.86)
  Pallas kernels: 122 us -> 109 us
  local copies, waits for them, and re-layouts: 5.86 us -> 0 us
    pallas_call x1 -> x2, Pallas kernels: 122 us -> 109 us  [the longest x1 108 us: shards(): pl.pallas_call(functools.partial(kernel, nz, nx, nt), out_shape=tuple((V(...]
    unnamed x6 -> x0, local copies, waits for them, and re-layouts: 5.86 us -> none
where the time goes in v3:
time: 111 us; the launch traced here: 110 us
  Pallas kernels  109 us (98%)
    pallas_call x1, Pallas kernels, shards(): pl.pallas_call(functools.partial(kernel, nz, nx, nt), out_shape=tuple((V(...  108 us

profile of v3, /device:TPU:2, one launch (start us, length us, event | category | flops | bytes accessed | tf_op | source)
XLA Modules:
  0.0 109.9 jit_solution(17065441904353751008)
XLA Ops:
  0.6 108.2 %step.1 = (bf16[2,4096]{1,0:T(2,128)(2,1)S(1)}, bf16[3,32,512]{2,1,0:T(8,128)(2,1)S(1)}, f32[32,16,512]{2,1,0:T(8,128)S(1)}, bf16[64,768]{1,0:T(8,128)(2,1)S(1)}) custom-call(bf16[2,4096]{1,0:T(2,128)(2,1)} %tokens.1, bf16[2,16]{1,0:T(2,128)(2,1)} %norm_gains.1, bf16[4,32]{1,0:T(4,128)(2,1)} %conv_weight.1, bf16[2,32]{1,0:T(2,128)(2,1)} %conv_skip.1, ...), custom_call_target="tpu_custom_call" | custom-call | tf_op jit(solution)/shard_map/step/pallas_call | solution.py:482
  108.8 1.1 write_out.1

commit v4 on v3

--- a/solution.py
+++ b/solution.py
@@ -19,8 +19,8 @@
 
 PHASES = (
     "x1", "xb", "rs", "wi0", "wi1", "gn", "rg", "prz", "sez", "x2",
-    "st", "wo", "we0", "we1", "stz", "p3x0", "p3x1", "p3z0", "p3z1", "prx",
-    "sex", "pr2", "stx", "gnx", "rgx", "wox", "wex", "sel", "gz", "mc",
+    "st", "wo", "we0", "we1", "we2", "stz", "p3x0", "p3x1", "p3z0", "p3z1", "prx",
+    "sex", "pr2", "stx", "gnx", "rgx", "wox", "wex0", "wex1", "wex2", "sel", "gz", "mc",
     "y2", "yo", "info", "lz", "ysx", "y2b", "yx1", "yx2", "yx3", "ez0",
     "ez1", "ez2", "ez3", "fin",
 )
@@ -62,7 +62,7 @@
     mamba_out, conv_next, ssm_next, expert_hidden,
     input_proj, select_t, output_t, expert_proj, conv_state, ssm_state,
     x1, xb, x2, xx, rs_s, rs_r, wi_s, wi_r, gn_s, gn_r, gn_b, gn_x, rg_s, rg_r, rg_b, rg_x, wo_r, wo_x,
-    st_s, st_r, st_b, st_z, st_x, pk, pr_s, pr_z, pr_x, pr2, se_s, se_z, se_x, p3, p3x, p3zs, p3z,
+    st_r, st_b, st_z, st_x, pk, pr_s, pr_z, pr_x, pr2, se_s, se_z, se_x, p3, p3x, p3zs, p3z,
     we_s, we_r, we_x, sel_s, sel_r, maps, step_b, act_b, ro_b, ga_s, g_z,
     mo_s, mc_r, y_s, y2, ysx, y2b, yo, yx, info_s, info_r, lg, lgz, pe, pez, fin_s, fin,
     ssem, rsem, lsem,
@@ -79,6 +79,7 @@
     rq = td * nt
     rank = nr * nt
     hid = expert_proj.shape[3] // nt
+    pieces, hc = we_r.shape[0], we_r.shape[4]
     cdev = conv_weight.shape[1]
     per_x = 4 // nx
     groups = {
@@ -142,13 +143,34 @@
 
     gn_s[...] = jnp.zeros(gn_s.shape, bf16)
     gn_s[:, 0:rows] = norm_gains[...]
-    loads["input"].wait()
+
+    def send_input(j):
+        wi_s[j] = input_proj[:, j, :]
+        send("tp", "wi%d" % j, lambda p: cols(wi_s.at[j], p, ch), wi_r.at[j])
+
+    def send_experts(e):
+        dst = we_r.at[e]
+        send(
+            "tp", "we%d" % e,
+            lambda p: we_s.at[:, :, pl.ds(pl.multiple_of(p * hid + e * hc, hc), hc)], dst,
+            at=lambda me: dst.at[:, me], part=dst.at[:, pl.ds(0, nt - 1)],
+        )
+
+    def pass_experts(e):
+        arrived("we%d" % e, we_r.at[e])
+        send("x", "wex%d" % e, lambda p: we_r.at[e, pl.ds(p * per_x, per_x)], we_x.at[e])
+
+    def lay_experts(e):
+        for j in range(2):
+            we_s[2 * e + j] = expert_proj[:, e, j, :]
+
+    xf = tokens[...].astype(f32)
+    rs = lax.rsqrt(jnp.mean(xf * xf, axis=1, keepdims=True) + EPS)
+    rs_s[...] = jnp.broadcast_to(rs, (td, LANES))
     pl.semaphore_wait(barrier, nt - 1 + nr - 1)
     send("rep", "x1", lambda p: cols(tokens, p, fb), x1)
     send("tp", "gn", lambda p: gn_s, gn_r)
-    for j in range(2):
-        wi_s[j] = input_proj[:, j, :]
-        send("tp", "wi%d" % j, lambda p, j=j: cols(wi_s.at[j], p, ch), wi_r.at[j])
+    send("tp", "rs", lambda p: rs_s, rs_r)
     pk[...] = jnp.zeros(pk.shape, f32)
     pk[0:4, 0:cdev] = conv_weight[...].astype(f32)
     pk[4:6, 0:cdev] = conv_skip[...].astype(f32)
@@ -160,37 +182,29 @@
     loads["select"].wait()
     se_s[0 : select_t.shape[0], :] = select_t[...]
     send("z", "sez", lambda p: se_s, se_z)
-    send("z", "xb", lambda p: cols(tokens, p, fz), xb)
-    at_row = lax.broadcasted_iota(jnp.int32, (nt, 1), 0) == t
-    st_s[...] = jnp.where(at_row, step_row[...].astype(f32), 0.0).astype(bf16)
+    loads["input"].wait()
+    send_input(0)
+    rg_s[...] = jnp.zeros(rg_s.shape, bf16)
+    rg_s[:, 0 : router.shape[1]] = router[...]
     arrived("x1", x1)
     send("tp", "x2", lambda p: x1, x2)
-    send("tp", "st", lambda p: cols(st_s, p, ch), st_r)
-    xf = tokens[...].astype(f32)
-    rs = lax.rsqrt(jnp.mean(xf * xf, axis=1, keepdims=True) + EPS)
-    rs_s[...] = jnp.broadcast_to(rs, (td, LANES))
-    send("tp", "rs", lambda p: rs_s, rs_r)
-    rg_s[...] = jnp.zeros(rg_s.shape, bf16)
-    rg_s[:, 0 : router.shape[1]] = router[...]
-    send("tp", "rg", lambda p: rg_s, rg_r)
-
-    def send_experts(e):
-        for j in range(2):
-            we_s[2 * e + j] = expert_proj[:, e, j, :]
-        half = we_r.at[pl.ds(2 * e, 2)]
-        send(
-            "tp", "we%d" % e,
-            lambda p: we_s.at[pl.ds(2 * e, 2), :, pl.ds(pl.multiple_of(p * hid, hid), hid)], half,
-            at=lambda me: half.at[:, me], part=half.at[:, pl.ds(0, nt - 1)],
-        )
-
-    arrived("prz", pr_z)
-    send("x", "prx", lambda p: pr_z, pr_x)
+    send_input(1)
+    send("tp", "st", lambda p: cols(step_row, p, ch), st_r)
+    loads["output"].wait()
+    send("tp", "wo", lambda p: cols(output_t, p, ch), wo_r)
+    send("z", "xb", lambda p: cols(tokens, p, fz), xb)
+    loads["expert"].wait()
+    lay_experts(0)
+
     arrived("gn", gn_r)
     gnv = gn_r[...].astype(f32)
     gains = jnp.concatenate([gnv[k][:, 0:rows] for k in range(nt)], axis=1)
     gn_b[...] = gains.astype(bf16)
     gain0 = gains[0:1, :]
+    arrived("prz", pr_z)
+    send("x", "prx", lambda p: pr_z, pr_x)
+    arrived("sez", se_z)
+    send("x", "sex", lambda p: se_z, se_x)
     arrived("x2", x2)
 
     def place_in(q, carry):
@@ -216,30 +230,23 @@
     partial_in(0)
     send_in(0)
 
-    arrived("st", st_r)
-    st_b[...] = jnp.sum(st_r[...].astype(f32), axis=0).astype(bf16)
-    send("z", "stz", lambda p: st_b, st_z)
-    arrived("sez", se_z)
-    send("x", "sex", lambda p: se_z, se_x)
-    partial_in(1)
     arrived("prx", pr_x)
     send("tp", "pr2", lambda p: pr_x.at[p % nx, p // nx], pr2)
-    loads["output"].wait()
-    send("tp", "wo", lambda p: cols(output_t, p, ch), wo_r)
-    loads["expert"].wait()
+    partial_in(1)
+    send_in(1)
+    arrived("st", st_r)
+    st_b[...] = st_r[...].astype(f32).reshape(nt, ch).astype(bf16)
+    send("z", "stz", lambda p: st_b, st_z)
+    lay_experts(1)
     send_experts(0)
+    sum_in(0)
+    send("tp", "rg", lambda p: rg_s, rg_r)
     arrived("stz", st_z)
     send("x", "stx", lambda p: st_z, st_x)
-    send_in(1)
-    sum_in(0)
-    send_experts(1)
-    arrived("rg", rg_r)
-    rgt = rg_r[...].reshape(fb, LANES).astype(f32).T
-    rg_b[...] = rgt[0 : rg_b.shape[0]].astype(bf16)
-    send("x", "gnx", lambda p: gn_b, gn_x)
-    send("x", "rgx", lambda p: rg_b, rg_x)
     arrived("wo", wo_r)
     send("x", "wox", lambda p: wo_r, wo_x)
+    send("x", "gnx", lambda p: gn_b, gn_x)
+    sum_in(1)
     arrived("sex", se_x)
     srw = se_s.shape[0]
     sp = sel_s.shape[1]
@@ -251,8 +258,6 @@
     true_col = ((blk % nz) * nx + blk // nz) * width + off
     perm = jnp.where((true_col == at_col) & (off < width), 1.0, 0.0).astype(bf16)
     select_all = dot(perm, se_x[...].reshape(nr * srw, ch)).astype(bf16)
-    arrived("rs", rs_r)
-    rsv = rs_r[...].reshape(rq, LANES)[:, 0:1]
     arrived("pr2", pr2)
     prv = pr2[...].astype(f32)
     par = jnp.concatenate([prv[k][:, 0:cdev] for k in range(nt)], axis=1)
@@ -261,6 +266,8 @@
     decay_rate = -jnp.exp(par[7 : 7 + st])
     conv_next[0] = conv_state[1]
     conv_next[1] = conv_state[2]
+    arrived("rs", rs_r)
+    rsv = rs_r[...].reshape(rq, LANES)[:, 0:1]
     arrived("p3z0", p3z.at[0])
     conv_input = total(p3z.at[0]) * rsv
     conv_next[2] = conv_input.astype(bf16)
@@ -268,10 +275,13 @@
     sel_s[...] = dot_nt(activated.astype(bf16), select_all).astype(bf16)
     send("tp", "sel", lambda p: sel_s, sel_r)
     act_b[...] = activated
-    sum_in(1)
-    for e in range(2):
-        arrived("we%d" % e, we_r.at[pl.ds(2 * e, 2)])
-    send("x", "wex", lambda p: we_r.at[pl.ds(p * per_x, per_x)], we_x)
+    if pieces > 1:
+        send_experts(1)
+    arrived("rg", rg_r)
+    rgt = rg_r[...].reshape(fb, LANES).astype(f32).T
+    rg_b[...] = rgt[0 : rg_b.shape[0]].astype(bf16)
+    send("x", "rgx", lambda p: rg_b, rg_x)
+    pass_experts(0)
     loads["ssm"].wait()
     arrived("stx", st_x)
     step_all = jnp.concatenate([st_x[q % nx, q // nx] for q in range(nr)], axis=0)
@@ -298,11 +308,17 @@
     ga_s[...] = (readout * silu(gate_z)).astype(bf16)
 
     send("z", "gz", lambda p: ga_s, g_z)
+    for e in range(2, pieces):
+        send_experts(e)
+    if pieces > 1:
+        pass_experts(1)
     arrived("wox", wo_x)
     arrived("gz", g_z)
     mo = dot_nt(g_z[...].reshape(nz * rq, ch), wo_x[...].reshape(fz, ch))
     mo_s[...] = mo.astype(bf16).reshape(nz, nt, td, fz)
     send("tp", "mc", lambda p: mo_s.at[:, p], mc_r)
+    for e in range(2, pieces):
+        pass_experts(e)
     arrived("xb", xb)
     arrived("mc", mc_r)
     y_s[...] = (xb[...].astype(f32) + total(mc_r)).astype(bf16)
@@ -318,37 +334,36 @@
     arrived("rgx", rg_x)
     experts = rg_b.shape[0]
     router_all = jnp.concatenate([rg_x[k] for k in range(nx)], axis=1)
-    if relay:
-        arrived("ysx", ysx)
-        send("tp", "y2b", lambda p: ysx, y2b)
 
     def place_out(src, k):
         for q in range(nz):
             block = src[:, q].reshape(rq, fz).astype(f32)
             yx[k, q] = (block * gain1).astype(bf16)
 
+    if relay:
+        arrived("ysx", ysx)
+        send("tp", "y2b", lambda p: ysx, y2b)
     arrived("y2", y2)
     place_out(y2, 0)
     for k in range(1, nx):
         if k != relay:
             remote(yx.at[0], yx.at[k], PH["yx%d" % k], {"rep_1": (x + k) % nx})
             pending.append((PH["yx%d" % k], yx.at[0]))
-    arrived("wex", we_x)
-    order = [0] + ([relay] if relay else []) + [k for k in range(1, nx) if k != relay]
-    for k in order:
-        if relay and k == relay:
-            arrived("y2b", y2b)
-            place_out(y2b, k)
-        elif k:
-            arrived("yx%d" % k, yx.at[k])
+    for e in range(pieces):
+        arrived("wex%d" % e, we_x.at[e])
+
+    def multiply(k):
         left = yx[k].reshape(nz * rq, fz)
         for c in range(per_x):
-            part = dot(left, we_x[:, c].reshape(fz, hid))
-            pe[k, :, c] = part.astype(bf16).reshape(nz, rq, hid)
-        send("z", "ez%d" % k, lambda p, k=k: pe.at[k, p], pez.at[k])
-        if k == 0:
-            lg[:, :, 0:experts] = dot_nt(left, router_all).astype(bf16).reshape(nz, rq, experts)
-            send("z", "lz", lambda p: lg.at[p], lgz)
+            for e in range(pieces):
+                part = dot(left, we_x[e, :, c].reshape(fz, hc))
+                pe[k, :, c, :, e * hc : (e + 1) * hc] = part.astype(bf16).reshape(nz, rq, hc)
+
+    multiply(0)
+    send("z", "ez0", lambda p: pe.at[0, p], pez.at[0])
+    left = yx[0].reshape(nz * rq, fz)
+    lg[:, :, 0:experts] = dot_nt(left, router_all).astype(bf16).reshape(nz, rq, experts)
+    send("z", "lz", lambda p: lg.at[p], lgz)
 
     arrived("yo", yo)
     yov = [yo[k].astype(f32) for k in range(nz)]
@@ -371,14 +386,21 @@
     info_s[...] = about
     send("tp", "info", lambda p: info_s, info_r)
 
+    order = ([relay] if relay else []) + [k for k in range(1, nx) if k != relay]
+    for k in order:
+        if relay and k == relay:
+            arrived("y2b", y2b)
+            place_out(y2b, k)
+        else:
+            arrived("yx%d" % k, yx.at[k])
+        multiply(k)
+        send("z", "ez%d" % k, lambda p, k=k: pe.at[k, p], pez.at[k])
     for k in order:
         arrived("ez%d" % k, pez.at[k])
-        done = total(pez.at[k]).astype(bf16)
-        if k == 0:
-            fin[pl.ds(x, 1)] = done[None]
-        else:
-            fin_s[k] = done
-            remote(fin_s.at[k], fin.at[x], PH["fin"], {"rep_1": (x + nx - k) % nx})
+        fin_s[k] = total(pez.at[k]).astype(bf16)
+        remote(fin_s.at[k], fin.at[x], PH["fin"], {"rep_1": (x + nx - k) % nx})
+    arrived("ez0", pez.at[0])
+    fin[pl.ds(x, 1)] = total(pez.at[0]).astype(bf16)[None]
 
     arrived("info", info_r)
     arrived("lz", lgz)
@@ -436,6 +458,8 @@
     sp = -(-width * nr // LANES) * LANES
     prw = -(-(7 + st) // 8) * 8
     per_x = 4 // nx
+    pieces = 3 if hid % (3 * LANES) == 0 else 2 if hid % 2 == 0 else 1
+    hc = hid // pieces
     oc = output_proj.shape[1]
 
     V = pltpu.VMEM
@@ -454,14 +478,15 @@
         rg_s=((rows, LANES), bf16), rg_r=((nt, rows, LANES), bf16), rg_b=((experts, fb), bf16),
         rg_x=((nx, experts, fb), bf16),
         wo_r=((nt, oc, ch), bf16), wo_x=((nx, nt, oc, ch), bf16),
-        st_s=((nt, nt * ch), bf16), st_r=((nt, nt, ch), bf16), st_b=((nt, ch), bf16),
+        st_r=((nt, 1, ch), bf16), st_b=((nt, ch), bf16),
         st_z=((nz, nt, ch), bf16), st_x=((nx, nz, nt, ch), bf16),
         pk=((prw, LANES), f32), pr_s=((prw, LANES), bf16), pr_z=((nz, prw, LANES), bf16),
         pr_x=((nx, nz, prw, LANES), bf16), pr2=((nt, prw, LANES), bf16),
         se_s=((srw, ch), bf16), se_z=((nz, srw, ch), bf16), se_x=((nx, nz, srw, ch), bf16),
         p3=((2, nx, nz, rq, ch), bf16), p3x=((2, nx, nz, rq, ch), bf16),
         p3zs=((2, nz, rq, ch), bf16), p3z=((2, nz, rq, ch), bf16),
-        we_s=((4, rows, nt * hid), bf16), we_r=((4, nt, rows, hid), bf16), we_x=((nx, per_x, nt, rows, hid), bf16),
+        we_s=((4, rows, nt * hid), bf16), we_r=((pieces, 4, nt, rows, hc), bf16),
+        we_x=((pieces, nx, per_x, nt, rows, hc), bf16),
         sel_s=((rq, sp), bf16), sel_r=((nt, rq, sp), bf16),
         maps=((rq, 2 * st, LANES), f32), step_b=((rq, ch), f32), act_b=((rq, ch), f32),
         ro_b=((rq, ch), f32),

time: 111 us -> 102 us (0.919)
  Pallas kernels: 109 us -> 99.4 us
    pallas_call x1, Pallas kernels: 108 us -> 98.4 us  [shards(): pl.pallas_call(functools.partial(kernel, nz, nx, nt), out_shape=tuple((V(...]
where the time goes in v4:
time: 102 us; the launch traced here: 100 us
  Pallas kernels  99.4 us (97%)
    pallas_call x1, Pallas kernels, shards(): pl.pallas_call(functools.partial(kernel, nz, nx, nt), out_shape=tuple((V(...  98.4 us

profile of v4, /device:TPU:2, one launch (start us, length us, event | category | flops | bytes accessed | tf_op | source)
XLA Modules:
  0.0 100.1 jit_solution(11045090697139477873)
XLA Ops:
  0.6 98.4 %step.1 = (bf16[2,4096]{1,0:T(2,128)(2,1)S(1)}, bf16[3,32,512]{2,1,0:T(8,128)(2,1)S(1)}, f32[32,16,512]{2,1,0:T(8,128)S(1)}, bf16[64,768]{1,0:T(8,128)(2,1)S(1)}) custom-call(bf16[2,4096]{1,0:T(2,128)(2,1)} %tokens.1, bf16[2,16]{1,0:T(2,128)(2,1)} %norm_gains.1, bf16[4,32]{1,0:T(4,128)(2,1)} %conv_weight.1, bf16[2,32]{1,0:T(2,128)(2,1)} %conv_skip.1, ...), custom_call_target="tpu_custom_call" | custom-call | tf_op jit(solution)/shard_map/step/pallas_call | solution.py:507
  99.0 1.1 %write_out.1 = (bf16[2,4096]{1,0:T(2,128)(2,1)}, bf16[3,32,512]{2,1,0:T(8,128)(2,1)}, f32[32,16,512]{2,1,0:T(8,128)}, bf16[64,768]{1,0:T(8,128)(2,1)}) custom-call(bf16[2,4096]{1,0:T(2,128)(2,1)S(1)} %get-tuple-element.8.refs_0_, bf16[3,32,512]{2,1,0:T(8,128)(2,1)S(1)} %get-tuple-element.9.refs_1_, f32[32,16,512]{2,1,0:T(8,128)S(1)} %get-tuple-element.10.refs_2_, ...), custom_call_target="tpu_custom_call" | custom-call | tf_op jit(solution)/shard_map/write_out/pallas_call | solution.py:519

commit v5 on v4

--- a/solution.py
+++ b/solution.py
@@ -20,8 +20,8 @@
 PHASES = (
     "x1", "xb", "rs", "wi0", "wi1", "gn", "rg", "prz", "sez", "x2",
     "st", "wo", "we0", "we1", "we2", "stz", "p3x0", "p3x1", "p3z0", "p3z1", "prx",
-    "sex", "pr2", "stx", "gnx", "rgx", "wox", "wex0", "wex1", "wex2", "sel", "gz", "mc",
-    "y2", "yo", "info", "lz", "ysx", "y2b", "yx1", "yx2", "yx3", "ez0",
+    "sex", "pr2", "stx", "gnx", "rgx", "wox", "wex0", "wex1", "wex2", "selp", "sel", "self", "gz", "mc",
+    "y2", "yo", "info", "lz", "yx1", "yx2", "yx3", "yx4", "wol", "wo1", "wo2", "wo3", "wo4", "ez0",
     "ez1", "ez2", "ez3", "fin",
 )
 PH = {name: k for k, name in enumerate(PHASES)}
@@ -63,8 +63,8 @@
     input_proj, select_t, output_t, expert_proj, conv_state, ssm_state,
     x1, xb, x2, xx, rs_s, rs_r, wi_s, wi_r, gn_s, gn_r, gn_b, gn_x, rg_s, rg_r, rg_b, rg_x, wo_r, wo_x,
     st_r, st_b, st_z, st_x, pk, pr_s, pr_z, pr_x, pr2, se_s, se_z, se_x, p3, p3x, p3zs, p3z,
-    we_s, we_r, we_x, sel_s, sel_r, maps, step_b, act_b, ro_b, ga_s, g_z,
-    mo_s, mc_r, y_s, y2, ysx, y2b, yo, yx, info_s, info_r, lg, lgz, pe, pez, fin_s, fin,
+    we_s, we_r, we_x, sel_s, sel_p, sel_h, sel_r, sel_f, maps, step_b, act_b, ro_b, ga_s, g_z,
+    mo_s, mc_r, y_s, y2, yo, yx, info_s, info_r, lg, lgz, pe, pez, fin_s, fin,
     ssem, rsem, lsem,
 ):
     nr = nz * nx
@@ -88,6 +88,9 @@
         "x": (nx, x, lambda p: {"rep_1": p}),
         "z": (nz, z, lambda p: {"rep_0": p}),
     }
+    core = t % 2
+    partner = {"tp": t + 1 - 2 * core}
+    groups["chip"] = (nt // 2, t // 2, lambda p: {"tp": p * 2 + core})
     pending = []
 
     def remote(src, dst, k, device):
@@ -171,6 +174,7 @@
     send("rep", "x1", lambda p: cols(tokens, p, fb), x1)
     send("tp", "gn", lambda p: gn_s, gn_r)
     send("tp", "rs", lambda p: rs_s, rs_r)
+    send("tp", "st", lambda p: cols(step_row, p, ch), st_r)
     pk[...] = jnp.zeros(pk.shape, f32)
     pk[0:4, 0:cdev] = conv_weight[...].astype(f32)
     pk[4:6, 0:cdev] = conv_skip[...].astype(f32)
@@ -189,22 +193,28 @@
     arrived("x1", x1)
     send("tp", "x2", lambda p: x1, x2)
     send_input(1)
-    send("tp", "st", lambda p: cols(step_row, p, ch), st_r)
     loads["output"].wait()
     send("tp", "wo", lambda p: cols(output_t, p, ch), wo_r)
     send("z", "xb", lambda p: cols(tokens, p, fz), xb)
+    arrived("st", st_r)
+    st_b[...] = st_r[...].astype(f32).reshape(nt, ch).astype(bf16)
+    send("z", "stz", lambda p: st_b, st_z)
+    arrived("prz", pr_z)
+    send("x", "prx", lambda p: pr_z, pr_x)
     loads["expert"].wait()
     lay_experts(0)
+    arrived("sez", se_z)
+    send("x", "sex", lambda p: se_z, se_x)
+    lay_experts(1)
+    arrived("prx", pr_x)
+    send("tp", "pr2", lambda p: pr_x.at[p % nx, p // nx], pr2)
+    send_experts(0)
 
     arrived("gn", gn_r)
     gnv = gn_r[...].astype(f32)
     gains = jnp.concatenate([gnv[k][:, 0:rows] for k in range(nt)], axis=1)
     gn_b[...] = gains.astype(bf16)
     gain0 = gains[0:1, :]
-    arrived("prz", pr_z)
-    send("x", "prx", lambda p: pr_z, pr_x)
-    arrived("sez", se_z)
-    send("x", "sex", lambda p: se_z, se_x)
     arrived("x2", x2)
 
     def place_in(q, carry):
@@ -230,23 +240,24 @@
     partial_in(0)
     send_in(0)
 
-    arrived("prx", pr_x)
-    send("tp", "pr2", lambda p: pr_x.at[p % nx, p // nx], pr2)
     partial_in(1)
     send_in(1)
-    arrived("st", st_r)
-    st_b[...] = st_r[...].astype(f32).reshape(nt, ch).astype(bf16)
-    send("z", "stz", lambda p: st_b, st_z)
-    lay_experts(1)
-    send_experts(0)
     sum_in(0)
-    send("tp", "rg", lambda p: rg_s, rg_r)
     arrived("stz", st_z)
     send("x", "stx", lambda p: st_z, st_x)
+    send("tp", "rg", lambda p: rg_s, rg_r)
     arrived("wo", wo_r)
-    send("x", "wox", lambda p: wo_r, wo_x)
+    right, left_x = {"rep_1": (x + 1) % nx}, {"rep_1": (x + nx - 1) % nx}
+    relay = nx == 4
+    oh = nt // 2
+    if relay:
+        remote(wo_r, wo_x.at[x], PH["wo1"], right)
+        remote(wo_r, wo_x.at[x], PH["wo2"], left_x)
+        pltpu.make_async_copy(wo_r, wo_x.at[x], rsem.at[PH["wol"]]).start()
+        pending.extend([(PH["wo1"], wo_r), (PH["wo2"], wo_r)])
+    else:
+        send("x", "wox", lambda p: wo_r, wo_x)
     send("x", "gnx", lambda p: gn_b, gn_x)
-    sum_in(1)
     arrived("sex", se_x)
     srw = se_s.shape[0]
     sp = sel_s.shape[1]
@@ -273,8 +284,15 @@
     conv_next[2] = conv_input.astype(bf16)
     activated = silu(history + par[3:4] * conv_input)
     sel_s[...] = dot_nt(activated.astype(bf16), select_all).astype(bf16)
-    send("tp", "sel", lambda p: sel_s, sel_r)
+    rh = rq // 2
+    mine = pl.ds(pl.multiple_of(core * rh, rh), rh)
+    remote(sel_s.at[pl.ds(pl.multiple_of((1 - core) * rh, rh), rh)], sel_p, PH["selp"], partner)
+    pending.append((PH["selp"], sel_p))
     act_b[...] = activated
+    arrived("selp", sel_p)
+    sel_h[...] = (sel_s[mine].astype(f32) + sel_p[...].astype(f32)).astype(bf16)
+    send("chip", "sel", lambda p: sel_h, sel_r)
+    sum_in(1)
     if pieces > 1:
         send_experts(1)
     arrived("rg", rg_r)
@@ -286,7 +304,20 @@
     arrived("stx", st_x)
     step_all = jnp.concatenate([st_x[q % nx, q // nx] for q in range(nr)], axis=0)
     arrived("sel", sel_r)
-    selected = total(sel_r)
+    sel_f[core] = total(sel_r)
+    remote(sel_f.at[core], sel_f.at[core], PH["self"], partner)
+    pending.append((PH["self"], sel_f.at[0]))
+    if relay:
+        from_left, from_right = wo_x.at[(x + 3) % nx], wo_x.at[(x + 1) % nx]
+        arrived("wo1", from_left)
+        arrived("wo2", from_right)
+        for name, part, to in (
+            ("wo3", from_left.at[pl.ds(0, oh)], right), ("wo4", from_right.at[pl.ds(oh, oh)], left_x),
+        ):
+            remote(part, part, PH[name], to)
+            pending.append((PH[name], part))
+    arrived("self", sel_f.at[0])
+    selected = jnp.concatenate([sel_f[0], sel_f[1]], axis=0)
     step_low = selected[:, :rank].astype(bf16)
     maps[...] = jnp.broadcast_to(selected[:, rank : rank + 2 * st][:, :, None], maps.shape)
     step_b[...] = softplus(dot(step_low, step_all) + par[6:7])
@@ -312,7 +343,12 @@
         send_experts(e)
     if pieces > 1:
         pass_experts(1)
-    arrived("wox", wo_x)
+    if relay:
+        arrived("wol", wo_x.at[x])
+        arrived("wo3", wo_x.at[(x + 2) % nx, pl.ds(0, oh)])
+        arrived("wo4", wo_x.at[(x + 2) % nx, pl.ds(oh, oh)])
+    else:
+        arrived("wox", wo_x)
     arrived("gz", g_z)
     mo = dot_nt(g_z[...].reshape(nz * rq, ch), wo_x[...].reshape(fz, ch))
     mo_s[...] = mo.astype(bf16).reshape(nz, nt, td, fz)
@@ -322,10 +358,6 @@
     arrived("xb", xb)
     arrived("mc", mc_r)
     y_s[...] = (xb[...].astype(f32) + total(mc_r)).astype(bf16)
-    relay = nx // 2 if nx > 2 else 0
-    if relay:
-        remote(y_s, ysx, PH["ysx"], {"rep_1": (x + relay) % nx})
-        pending.append((PH["ysx"], ysx))
     send("tp", "y2", lambda p: y_s, y2)
     send("z", "yo", lambda p: y_s.at[p], yo)
 
@@ -340,15 +372,11 @@
             block = src[:, q].reshape(rq, fz).astype(f32)
             yx[k, q] = (block * gain1).astype(bf16)
 
-    if relay:
-        arrived("ysx", ysx)
-        send("tp", "y2b", lambda p: ysx, y2b)
     arrived("y2", y2)
     place_out(y2, 0)
-    for k in range(1, nx):
-        if k != relay:
-            remote(yx.at[0], yx.at[k], PH["yx%d" % k], {"rep_1": (x + k) % nx})
-            pending.append((PH["yx%d" % k], yx.at[0]))
+    for k in (1, 3) if relay else range(1, nx):
+        remote(yx.at[0], yx.at[k], PH["yx%d" % k], {"rep_1": (x + k) % nx})
+        pending.append((PH["yx%d" % k], yx.at[0]))
     for e in range(pieces):
         arrived("wex%d" % e, we_x.at[e])
 
@@ -386,13 +414,19 @@
     info_s[...] = about
     send("tp", "info", lambda p: info_s, info_r)
 
-    order = ([relay] if relay else []) + [k for k in range(1, nx) if k != relay]
+    order = (1, 3, 2) if relay else tuple(range(1, nx))
+    first_rows, last_rows = pl.ds(0, rq // 2), pl.ds(rq // 2, rq // 2)
+    passed = {1: ("yx2", first_rows, right), 3: ("yx4", last_rows, left_x)}
     for k in order:
-        if relay and k == relay:
-            arrived("y2b", y2b)
-            place_out(y2b, k)
+        if relay and k == 2:
+            arrived("yx2", yx.at[2, :, first_rows])
+            arrived("yx4", yx.at[2, :, last_rows])
         else:
             arrived("yx%d" % k, yx.at[k])
+        if relay and k in passed:
+            name, some, to = passed[k]
+            remote(yx.at[k, :, some], yx.at[2, :, some], PH[name], to)
+            pending.append((PH[name], yx.at[2, :, some]))
         multiply(k)
         send("z", "ez%d" % k, lambda p, k=k: pe.at[k, p], pez.at[k])
     for k in order:
@@ -487,12 +521,13 @@
         p3zs=((2, nz, rq, ch), bf16), p3z=((2, nz, rq, ch), bf16),
         we_s=((4, rows, nt * hid), bf16), we_r=((pieces, 4, nt, rows, hc), bf16),
         we_x=((pieces, nx, per_x, nt, rows, hc), bf16),
-        sel_s=((rq, sp), bf16), sel_r=((nt, rq, sp), bf16),
+        sel_s=((rq, sp), bf16), sel_p=((rq // 2, sp), bf16), sel_h=((rq // 2, sp), bf16),
+        sel_r=((nt // 2, rq // 2, sp), bf16), sel_f=((2, rq // 2, sp), f32),
         maps=((rq, 2 * st, LANES), f32), step_b=((rq, ch), f32), act_b=((rq, ch), f32),
         ro_b=((rq, ch), f32),
         ga_s=((rq, ch), bf16), g_z=((nz, rq, ch), bf16),
         mo_s=((nz, nt, td, fz), bf16), mc_r=((nt, nz, td, fz), bf16), y_s=((nz, td, fz), bf16),
-        y2=((nt, nz, td, fz), bf16), ysx=((nz, td, fz), bf16), y2b=((nt, nz, td, fz), bf16), yo=((nz, td, fz), bf16), yx=((nx, nz, rq, fz), bf16),
+        y2=((nt, nz, td, fz), bf16), yo=((nz, td, fz), bf16), yx=((nx, nz, rq, fz), bf16),
         info_s=((td, LANES), f32), info_r=((nt, td, LANES), f32),
         lg=((nz, rq, LANES), bf16), lgz=((nz, rq, LANES), bf16),
         pe=((nx, nz, per_x, rq, hid), bf16), pez=((nx, nz, per_x, rq, hid), bf16),

time: 102 us -> 102 us (level)
  no operation moved by 1% of the time
where the time goes in v5:
time: 102 us; the launch traced here: 100 us
  Pallas kernels  99.6 us (98%)
    pallas_call x1, Pallas kernels, shards(): pl.pallas_call(functools.partial(kernel, nz, nx, nt), out_shape=tuple((V(...  98.5 us

profile of v5, /device:TPU:2, one launch (start us, length us, event | category | flops | bytes accessed | tf_op | source)
XLA Modules:
  0.0 100.2 jit_solution(6799714723999916066)
XLA Ops:
  0.6 98.5 %step.1 = (bf16[2,4096]{1,0:T(2,128)(2,1)S(1)}, bf16[3,32,512]{2,1,0:T(8,128)(2,1)S(1)}, f32[32,16,512]{2,1,0:T(8,128)S(1)}, bf16[64,768]{1,0:T(8,128)(2,1)S(1)}) custom-call(bf16[2,4096]{1,0:T(2,128)(2,1)} %tokens.1, bf16[2,16]{1,0:T(2,128)(2,1)} %norm_gains.1, bf16[4,32]{1,0:T(4,128)(2,1)} %conv_weight.1, bf16[2,32]{1,0:T(2,128)(2,1)} %conv_skip.1, ...), custom_call_target="tpu_custom_call" | custom-call | tf_op jit(solution)/shard_map/step/pallas_call | solution.py:542
  99.2 1.1 %write_out.1 = (bf16[2,4096]{1,0:T(2,128)(2,1)}, bf16[3,32,512]{2,1,0:T(8,128)(2,1)}, f32[32,16,512]{2,1,0:T(8,128)}, bf16[64,768]{1,0:T(8,128)(2,1)}) custom-call(bf16[2,4096]{1,0:T(2,128)(2,1)S(1)} %get-tuple-element.8.refs_0_, bf16[3,32,512]{2,1,0:T(8,128)(2,1)S(1)} %get-tuple-element.9.refs_1_, f32[32,16,512]{2,1,0:T(8,128)S(1)} %get-tuple-element.10.refs_2_, ...), custom_call_target="tpu_custom_call" | custom-call | tf_op jit(solution)/shard_map/write_out/pallas_call | solution.py:554

commit v6 on v5

--- a/solution.py
+++ b/solution.py
@@ -21,8 +21,9 @@
     "x1", "xb", "rs", "wi0", "wi1", "gn", "rg", "prz", "sez", "x2",
     "st", "wo", "we0", "we1", "we2", "stz", "p3x0", "p3x1", "p3z0", "p3z1", "prx",
     "sex", "pr2", "stx", "gnx", "rgx", "wox", "wex0", "wex1", "wex2", "selp", "sel", "self", "gz", "mc",
-    "y2", "yo", "info", "lz", "yx1", "yx2", "yx3", "yx4", "wol", "wo1", "wo2", "wo3", "wo4", "ez0",
-    "ez1", "ez2", "ez3", "fin",
+    "y2", "yo", "info", "lz", "yx1a", "yx1b", "yx3a", "yx3b", "yx2a", "yx2b",
+    "wol", "wo1", "wo2", "wo3", "wo4", "ez0",
+    "ez1a", "ez1b", "ez2a", "ez2b", "ez3a", "ez3b", "fin",
 )
 PH = {name: k for k, name in enumerate(PHASES)}
 
@@ -374,20 +375,25 @@
 
     arrived("y2", y2)
     place_out(y2, 0)
-    for k in (1, 3) if relay else range(1, nx):
-        remote(yx.at[0], yx.at[k], PH["yx%d" % k], {"rep_1": (x + k) % nx})
-        pending.append((PH["yx%d" % k], yx.at[0]))
+    near = (1, 3) if relay else tuple(range(1, nx))
+    rh = rq // 2
+    halves = {"a": pl.ds(0, rh), "b": pl.ds(rh, rh)}
+    for half, some in halves.items():
+        for k in near:
+            name = "yx%d%s" % (k, half)
+            remote(yx.at[0, :, some], yx.at[k, :, some], PH[name], {"rep_1": (x + k) % nx})
+            pending.append((PH[name], yx.at[0, :, some]))
     for e in range(pieces):
         arrived("wex%d" % e, we_x.at[e])
 
-    def multiply(k):
-        left = yx[k].reshape(nz * rq, fz)
+    def multiply(k, some):
+        left = yx[k, :, some].reshape(nz * some.size, fz)
         for c in range(per_x):
             for e in range(pieces):
                 part = dot(left, we_x[e, :, c].reshape(fz, hc))
-                pe[k, :, c, :, e * hc : (e + 1) * hc] = part.astype(bf16).reshape(nz, rq, hc)
-
-    multiply(0)
+                pe[k, :, c, some, e * hc : (e + 1) * hc] = part.astype(bf16).reshape(nz, some.size, hc)
+
+    multiply(0, pl.ds(0, rq))
     send("z", "ez0", lambda p: pe.at[0, p], pez.at[0])
     left = yx[0].reshape(nz * rq, fz)
     lg[:, :, 0:experts] = dot_nt(left, router_all).astype(bf16).reshape(nz, rq, experts)
@@ -414,23 +420,26 @@
     info_s[...] = about
     send("tp", "info", lambda p: info_s, info_r)
 
-    order = (1, 3, 2) if relay else tuple(range(1, nx))
-    first_rows, last_rows = pl.ds(0, rq // 2), pl.ds(rq // 2, rq // 2)
-    passed = {1: ("yx2", first_rows, right), 3: ("yx4", last_rows, left_x)}
+    order = (1, 3, 2) if relay else near
+
+    def block(k, half):
+        some = halves[half]
+        arrived("yx%d%s" % (k, half), yx.at[k, :, some])
+        if relay and (k, half) in ((1, "a"), (3, "b")):
+            remote(yx.at[k, :, some], yx.at[2, :, some], PH["yx2" + half], right if k == 1 else left_x)
+            pending.append((PH["yx2" + half], yx.at[2, :, some]))
+        multiply(k, some)
+        send("z", "ez%d%s" % (k, half), lambda p: pe.at[k, p, :, some], pez.at[k, :, :, some])
+
+    for half in halves:
+        for k in near:
+            block(k, half)
+    if relay:
+        for half in halves:
+            block(2, half)
     for k in order:
-        if relay and k == 2:
-            arrived("yx2", yx.at[2, :, first_rows])
-            arrived("yx4", yx.at[2, :, last_rows])
-        else:
-            arrived("yx%d" % k, yx.at[k])
-        if relay and k in passed:
-            name, some, to = passed[k]
-            remote(yx.at[k, :, some], yx.at[2, :, some], PH[name], to)
-            pending.append((PH[name], yx.at[2, :, some]))
-        multiply(k)
-        send("z", "ez%d" % k, lambda p, k=k: pe.at[k, p], pez.at[k])
-    for k in order:
-        arrived("ez%d" % k, pez.at[k])
+        for half, some in halves.items():
+            arrived("ez%d%s" % (k, half), pez.at[k, :, :, some])
         fin_s[k] = total(pez.at[k]).astype(bf16)
         remote(fin_s.at[k], fin.at[x], PH["fin"], {"rep_1": (x + nx - k) % nx})
     arrived("ez0", pez.at[0])

time: 102 us -> 99.5 us (0.975)
  Pallas kernels: 99.6 us -> 97.8 us
    pallas_call x1, Pallas kernels: 98.5 us -> 96.8 us  [shards(): pl.pallas_call(functools.partial(kernel, nz, nx, nt), out_shape=tuple((V(...]
where the time goes in v6:
time: 99.5 us; the launch traced here: 98.5 us
  Pallas kernels  97.8 us (98%)
    pallas_call x1, Pallas kernels, shards(): pl.pallas_call(functools.partial(kernel, nz, nx, nt), out_shape=tuple((V(...  96.8 us

profile of v6, /device:TPU:2, one launch (start us, length us, event | category | flops | bytes accessed | tf_op | source)
XLA Modules:
  0.0 98.5 jit_solution(3707354695114400575)
XLA Ops:
  0.6 96.8 %step.1 = (bf16[2,4096]{1,0:T(2,128)(2,1)S(1)}, bf16[3,32,512]{2,1,0:T(8,128)(2,1)S(1)}, f32[32,16,512]{2,1,0:T(8,128)S(1)}, bf16[64,768]{1,0:T(8,128)(2,1)S(1)}) custom-call(bf16[2,4096]{1,0:T(2,128)(2,1)} %tokens.1, bf16[2,16]{1,0:T(2,128)(2,1)} %norm_gains.1, bf16[4,32]{1,0:T(4,128)(2,1)} %conv_weight.1, bf16[2,32]{1,0:T(2,128)(2,1)} %conv_skip.1, ...), custom_call_target="tpu_custom_call" | custom-call | tf_op jit(solution)/shard_map/step/pallas_call | solution.py:551
  97.4 1.1 %write_out.1 = (bf16[2,4096]{1,0:T(2,128)(2,1)}, bf16[3,32,512]{2,1,0:T(8,128)(2,1)}, f32[32,16,512]{2,1,0:T(8,128)}, bf16[64,768]{1,0:T(8,128)(2,1)}) custom-call(bf16[2,4096]{1,0:T(2,128)(2,1)S(1)} %get-tuple-element.8.refs_0_, bf16[3,32,512]{2,1,0:T(8,128)(2,1)S(1)} %get-tuple-element.9.refs_1_, f32[32,16,512]{2,1,0:T(8,128)S(1)} %get-tuple-element.10.refs_2_, ...), custom_call_target="tpu_custom_call" | custom-call | tf_op jit(solution)/shard_map/write_out/pallas_call | solution.py:563

commit v7 on v6

--- a/solution.py
+++ b/solution.py
@@ -440,8 +440,10 @@
     for k in order:
         for half, some in halves.items():
             arrived("ez%d%s" % (k, half), pez.at[k, :, :, some])
-        fin_s[k] = total(pez.at[k]).astype(bf16)
-        remote(fin_s.at[k], fin.at[x], PH["fin"], {"rep_1": (x + nx - k) % nx})
+            fin_s[k, :, some] = total(pez.at[k, :, :, some]).astype(bf16)
+            remote(
+                fin_s.at[k, :, some], fin.at[x, :, some], PH["fin"], {"rep_1": (x + nx - k) % nx}
+            )
     arrived("ez0", pez.at[0])
     fin[pl.ds(x, 1)] = total(pez.at[0]).astype(bf16)[None]
 

time: 99.5 us -> 99.2 us (level)
  no operation moved by 1% of the time
where the time goes in v7:
time: 99.2 us; the launch traced here: 98.2 us
  Pallas kernels  97.6 us (98%)
    pallas_call x1, Pallas kernels, shards(): pl.pallas_call(functools.partial(kernel, nz, nx, nt), out_shape=tuple((V(...  96.5 us

profile of v7, /device:TPU:2, one launch (start us, length us, event | category | flops | bytes accessed | tf_op | source)
XLA Modules:
  0.0 98.2 jit_solution(1427807991232686865)
XLA Ops:
  0.6 96.5 %step.1 = (bf16[2,4096]{1,0:T(2,128)(2,1)S(1)}, bf16[3,32,512]{2,1,0:T(8,128)(2,1)S(1)}, f32[32,16,512]{2,1,0:T(8,128)S(1)}, bf16[64,768]{1,0:T(8,128)(2,1)S(1)}) custom-call(bf16[2,4096]{1,0:T(2,128)(2,1)} %tokens.1, bf16[2,16]{1,0:T(2,128)(2,1)} %norm_gains.1, bf16[4,32]{1,0:T(4,128)(2,1)} %conv_weight.1, bf16[2,32]{1,0:T(2,128)(2,1)} %conv_skip.1, ...), custom_call_target="tpu_custom_call" | custom-call | tf_op jit(solution)/shard_map/step/pallas_call | solution.py:553
  97.1 1.1 %write_out.1 = (bf16[2,4096]{1,0:T(2,128)(2,1)}, bf16[3,32,512]{2,1,0:T(8,128)(2,1)}, f32[32,16,512]{2,1,0:T(8,128)}, bf16[64,768]{1,0:T(8,128)(2,1)}) custom-call(bf16[2,4096]{1,0:T(2,128)(2,1)S(1)} %get-tuple-element.8.refs_0_, bf16[3,32,512]{2,1,0:T(8,128)(2,1)S(1)} %get-tuple-element.9.refs_1_, f32[32,16,512]{2,1,0:T(8,128)S(1)} %get-tuple-element.10.refs_2_, ...), custom_call_target="tpu_custom_call" | custom-call | tf_op jit(solution)/shard_map/write_out/pallas_call | solution.py:565
